TPU v7x, 32 devices: a whole 2x2x4 slice. The times are simulated.
32 devices in a mesh: shift: 2 (over y), expert: 4 (over z), shard: 4 (over x, core).
Axes of the slice: x: 2, y: 2, z: 4, core: 2. Of those that a mesh axis runs over, the one named last changes fastest.
Arguments:
- master_gate: float32 [128, 2048, 1024], P(('shift', 'expert'), 'shard'), parts along dimension 0, may hold values from -0.1875 to 0.1875
- master_up: float32 [128, 2048, 1024], P(('shift', 'expert'), 'shard'), parts along dimension 0, may hold values from -0.1875 to 0.1875
- router_weight: float32 [4096, 64], P(('shift', 'shard'), 'expert'), parts along dimension 0, may hold values from -0.125 to 0.125
- router_gain: float32 [4096], P(('shift', 'shard')), parts along dimension 0, may hold values from 0.25 to 1.75
Outputs:
- final_gate: bfloat16 [128, 2048, 1024], P(('shift', 'expert'), None, 'shard'), parts along dimension 0
- final_up: bfloat16 [128, 2048, 1024], P(('shift', 'expert'), None, 'shard'), parts along dimension 0
- scale_gate: float32 [128, 1024], P(('shift', 'expert'), 'shard'), parts along dimension 0
- scale_up: float32 [128, 1024], P(('shift', 'expert'), 'shard'), parts along dimension 0
- serve_router: bfloat16 [4096, 64], P('shift'), parts along dimension 0
There are 2 independent parts, one for each index of `shift`. A program takes and returns all parts, laid end to end along the dimension named above; each array names one. Nothing has to cross between parts.
All inputs are finite; a program needn't handle non-finite values. Where the computation divides by a largest or mean magnitude, that divisor is 1e-20 or more.
Results may differ from a plain program's by a relative error of at most 0.001.
Values may be sent and summed in bfloat16 or wider, within the bound.
A program may use at most 256 MiB of HBM per device.

v0:
```python
import functools

import jax
import jax.numpy as jnp
from jax import lax
from jax.experimental import pallas as pl
from jax.experimental.pallas import tpu as pltpu
from jax.sharding import PartitionSpec as P

MESH = pl.DeviceIdType.MESH
LANES = 128
LAG = 6
AHEAD = 2
SLOTS = 5


def exchange(
    n, groups, gate, up, router, narrow, tail, scales, routers, held, out, mine, theirs,
    load_sem, max_send, max_recv, send_sem, recv_sem, keep_sem, rt_send, rt_recv, rt_keep,
):
    me, group = lax.axis_index("shard"), lax.axis_index("expert")
    items, rows, width, depth = 2 * gate.shape[0], gate.shape[1], out.shape[3], held.shape[0]
    blocks, per = gate.shape[2] // LANES, width // LANES
    others = [(j, g) for g in range(groups) for j in range(n) if (j, g) != (0, 0)]

    def peer(j):
        return lax.rem(me + j, n)

    def device(j, g):
        return {"shard": peer(j), "expert": lax.rem(group + g, groups)}

    def load(k):
        slot, expert = lax.rem(k, depth), k // 2

        @pl.when(lax.rem(k, 2) == 0)
        def _():
            pltpu.make_async_copy(gate.at[expert], held.at[slot], load_sem.at[slot]).start()

        @pl.when(lax.rem(k, 2) == 1)
        def _():
            pltpu.make_async_copy(up.at[expert], held.at[slot], load_sem.at[slot]).start()

    def send_max(k, j):
        return pltpu.make_async_remote_copy(
            mine.at[k], theirs.at[k, j - 1], max_send, max_recv.at[k],
            device_id=device(j, 0), device_id_type=MESH,
        )

    def place(k):
        return narrow.at[lax.rem(k, 2), k // 2, pl.ds(pl.multiple_of(me * rows, rows), rows)]

    def send(k, j):
        slot = lax.rem(k, SLOTS)
        return pltpu.make_async_remote_copy(
            out.at[slot, peer(j)], place(k), send_sem.at[slot], recv_sem.at[j - 1],
            device_id=device(j, 0), device_id_type=MESH,
        )

    def keep(k):
        slot = lax.rem(k, SLOTS)
        return pltpu.make_async_copy(out.at[slot, me], place(k), keep_sem.at[slot])

    def leave(k):
        slot = lax.rem(k, SLOTS)
        return pltpu.make_async_copy(out.at[slot], tail.at[:, lax.rem(k, 2)], keep_sem.at[slot])

    def sent(k):
        slot = lax.rem(k, SLOTS)
        ref = out.at[slot, pl.ds(0, n - 1)]
        pltpu.make_async_copy(ref, ref, send_sem.at[slot]).wait()
        keep(k).wait()

    for k in range(AHEAD):
        load(jnp.int32(k))
    barrier = pltpu.get_barrier_semaphore()
    for j, g in others:
        pl.semaphore_signal(barrier, inc=1, device_id=device(j, g), device_id_type=MESH)
    pl.semaphore_wait(barrier, len(others))

    home = routers.at[group * n + me]
    for j, g in others:
        pltpu.make_async_remote_copy(
            router, home, rt_send, rt_recv, device_id=device(j, g), device_id_type=MESH
        ).start()
    own = pltpu.make_async_copy(router, home, rt_keep)
    own.start()

    def step(k, _):
        @pl.when(k + AHEAD < items)
        def _():
            load(k + AHEAD)

        @pl.when(k < items)
        def _():
            slot = lax.rem(k, depth)
            pltpu.make_async_copy(gate.at[0], held.at[slot], load_sem.at[slot]).wait()
            for b in range(blocks):
                column = held[slot, :, b * LANES : (b + 1) * LANES]
                mine[k, b : b + 1, :] = jnp.max(jnp.abs(column), axis=0, keepdims=True)
            for j in range(1, n):
                send_max(k, j).start()

        q = k - LAG

        @pl.when(q >= 0)
        def _():
            @pl.when(q >= SLOTS)
            def _():
                sent(q - SLOTS)

            pltpu.make_async_copy(theirs.at[q], theirs.at[q], max_recv.at[q]).wait()
            scale = mine[q]
            for j in range(1, n):
                scale = jnp.maximum(scale, theirs[q, j - 1])
            scales[q] = scale
            slot, source = lax.rem(q, SLOTS), lax.rem(q, depth)
            for b in range(blocks):
                at = (b % per) * LANES
                column = held[source, :, b * LANES : (b + 1) * LANES]
                out[slot, b // per, :, at : at + LANES] = (column / scale[b : b + 1]).astype(
                    jnp.bfloat16
                )

            @pl.when(q < items - 2)
            def _():
                for j in range(1, n):
                    send(q, j).start()
                keep(q).start()

            @pl.when(q >= items - 2)
            def _():
                leave(q).start()

        return 0

    lax.fori_loop(0, items + LAG, step, 0)

    def drain(k, _):
        sent(k)
        return 0

    lax.fori_loop(items - SLOTS, items - 2, drain, 0)
    for k in (items - 2, items - 1):
        leave(jnp.int32(k)).wait()
    pltpu.make_async_copy(theirs, theirs, max_send).wait()
    for j in range(1, n):
        ref = narrow.at[:, :, pl.ds(pl.multiple_of(peer(n - j) * rows, rows), rows)]
        pltpu.make_async_copy(ref, ref, recv_sem.at[j - 1]).wait()
    rest = routers.at[pl.ds(0, n * groups - 1)]
    pltpu.make_async_copy(rest, rest, rt_send).wait()
    pltpu.make_async_copy(rest, rest, rt_recv).wait()
    own.wait()


def spread(narrow, gate, up):
    gate[...] = narrow[0]
    up[...] = narrow[1]


def finish(arrived, gate_in, up_in, gate, up):
    gate[...] = arrived[:, 0]
    up[...] = arrived[:, 1]


def by_kernel(n, groups, gate, up, router, gain):
    experts, rows, columns = gate.shape
    width, items, depth = columns // n, 2 * experts, LAG + AHEAD + 1
    tokens, share = router.shape
    part = (router * gain[:, None]).astype(jnp.bfloat16).reshape(-1, LANES)
    anywhere = pl.BlockSpec(memory_space=pl.ANY)
    inside = pl.BlockSpec(memory_space=pltpu.VMEM)
    dma = pltpu.SemaphoreType.DMA
    narrow, tail, scales, routers = pl.pallas_call(
        functools.partial(exchange, n, groups),
        name="exchange",
        out_shape=(
            jax.ShapeDtypeStruct((2, experts - 1, n * rows, width), jnp.bfloat16),
            jax.ShapeDtypeStruct((n, 2, rows, width), jnp.bfloat16),
            jax.ShapeDtypeStruct((items, columns // LANES, LANES), jnp.float32),
            jax.ShapeDtypeStruct((groups * n,) + part.shape, jnp.bfloat16),
        ),
        in_specs=[anywhere, anywhere, inside],
        out_specs=(anywhere, anywhere, inside, anywhere),
        scratch_shapes=[
            pltpu.VMEM((depth, rows, columns), jnp.float32),
            pltpu.VMEM((SLOTS, n, rows, width), jnp.bfloat16),
            pltpu.VMEM((items, columns // LANES, LANES), jnp.float32),
            pltpu.VMEM((items, n - 1, columns // LANES, LANES), jnp.float32),
            dma((depth,)),
            dma,
            dma((items,)),
            dma((SLOTS,)),
            dma((n - 1,)),
            dma((SLOTS,)),
            dma,
            dma,
            dma,
        ],
        compiler_params=pltpu.CompilerParams(collective_id=0, has_side_effects=True),
    )(gate, up, part)
    arrived = lax.all_to_all(tail, "shard", split_axis=0, concat_axis=0, tiled=True)
    finals = (jax.ShapeDtypeStruct((experts, n * rows, width), jnp.bfloat16),) * 2
    most = pl.pallas_call(
        spread,
        name="spread",
        grid=(experts - 1,),
        out_shape=finals,
        in_specs=[pl.BlockSpec((2, 1, n * rows, width), lambda e: (0, e, 0, 0))],
        out_specs=(pl.BlockSpec((1, n * rows, width), lambda e: (e, 0, 0)),) * 2,
        cost_estimate=pl.CostEstimate(flops=0, bytes_accessed=4 * narrow.size, transcendentals=0),
    )(narrow)
    final_gate, final_up = pl.pallas_call(
        finish,
        name="finish",
        grid=(n,),
        out_shape=finals,
        in_specs=[
            pl.BlockSpec((1, 2, rows, width), lambda s: (s, 0, 0, 0)), anywhere, anywhere,
        ],
        out_specs=(pl.BlockSpec((1, rows, width), lambda s: (experts - 1, s, 0)),) * 2,
        input_output_aliases={1: 0, 2: 1},
    )(arrived, *most)
    scales = lax.dynamic_slice_in_dim(
        scales.reshape(experts, 2, columns), lax.axis_index("shard") * width, width, axis=2
    )
    serve_router = routers.reshape(groups, n * tokens, share).transpose(1, 0, 2)
    return (
        final_gate, final_up, scales[:, 0], scales[:, 1],
        serve_router.reshape(n * tokens, groups * share),
    )


def by_collectives(gate, up, router, gain):
    scale_gate, scale_up = lax.pmax(
        (jnp.max(jnp.abs(gate), axis=1), jnp.max(jnp.abs(up), axis=1)), "shard"
    )

    def serve(master, scale):
        narrow = (master / jnp.expand_dims(scale, 1)).astype(jnp.bfloat16)
        final = lax.all_to_all(narrow, "shard", split_axis=2, concat_axis=1, tiled=True)
        width = final.shape[2]
        return final, lax.dynamic_slice_in_dim(
            scale, lax.axis_index("shard") * width, width, axis=1
        )

    final_gate, scale_gate = serve(gate, scale_gate)
    final_up, scale_up = serve(up, scale_up)
    part = (router * gain[:, None]).astype(jnp.bfloat16)
    rows = lax.all_gather(part, "shard", axis=0, tiled=True)
    return final_gate, final_up, scale_gate, scale_up, lax.all_gather(rows, "expert", axis=1, tiled=True)


def solution(mesh):
    n, groups = mesh.shape["shard"], mesh.shape["expert"]

    def shards(gate, up, router, gain):
        aligned = gate.shape[2] % (n * LANES) == 0 and gate.shape[1] % 16 == 0
        aligned = aligned and 2 * gate.shape[0] > SLOTS
        if n > 1 and aligned and router.size % (16 * LANES) == 0:
            return by_kernel(n, groups, gate, up, router, gain)
        return by_collectives(gate, up, router, gain)

    return jax.shard_map(
        shards,
        mesh=mesh,
        in_specs=(
            P(("shift", "expert"), "shard", None),
            P(("shift", "expert"), "shard", None),
            P(("shift", "shard"), "expert"),
            P(("shift", "shard")),
        ),
        out_specs=(
            P(("shift", "expert"), None, "shard"),
            P(("shift", "expert"), None, "shard"),
            P(("shift", "expert"), "shard"),
            P(("shift", "expert"), "shard"),
            P("shift", None),
        ),
        check_vma=False,
    )
```

profile of v0, /device:TPU:1, one launch (start us, length us, event | category | flops | bytes accessed | tf_op | source)
XLA Modules:
  0.0 400.2 jit_solution(11008754689263267707)
XLA Ops:
  0.6 0.8 multiply_convert_fusion
  1.4 0.1 copy.16
  1.5 0.7 reshape.23.router
  2.3 355.0 %exchange.1 = (bf16[2,15,2048,256]{3,2,1,0:T(8,128)(2,1)}, bf16[4,2,512,256]{3,2,1,0:T(8,128)(2,1)}, f32[32,8,128]{2,1,0:T(8,128)}, bf16[16,64,128]{2,1,0:T(8,128)(2,1)}) custom-call(f32[16,512,1024]{2,1,0:T(8,128)} %gate.1, f32[16,512,1024]{2,1,0:T(8,128)} %up.1, bf16[64,128]{1,0:T(8,128)(2,1)} %reshape.23.router), custom_call_target="tpu_custom_call" | custom-call | tf_op jit(solution)/shard_map/exchange/pallas_call | solution.py:173
  357.3 3.6 all-to-all-start
  360.9 1.0 reshape.24
  361.9 3.4 reshape.25
  365.3 2.5 copy.18
  367.8 26.5 %spread.1 = (bf16[16,2048,256]{2,1,0:T(8,128)(2,1)}, bf16[16,2048,256]{2,1,0:T(8,128)(2,1)}) custom-call(bf16[2,15,2048,256]{3,2,1,0:T(8,128)(2,1)} %get-tuple-element.14.narrow), custom_call_target="tpu_custom_call" | custom-call | bytes 62914560 | tf_op jit(solution)/shard_map/spread/pallas_call | solution.py:203
  394.3 0.1 constant_dynamic-slice_fusion.1
  394.4 0.6 copy_bitcast_fusion
  395.0 0.0 all-to-all-done.arrived
  395.0 0.0 copy-start
  395.0 1.3 copy-done
  396.4 3.8 finish.1
Async XLA Ops:
  357.3 37.8 %all-to-all-start = ((bf16[4,2,512,256]{3,2,1,0:T(8,128)(2,1)}), bf16[4,2,512,256]{3,2,1,0:T(8,128)(2,1)S(1)}, u32[]{:S(2)}, u32[]{:S(2)}) async-start(bf16[4,2,512,256]{3,2,1,0:T(8,128)(2,1)} %get-tuple-element.13), calls=%async_computation | async-start | bytes 4194304 | tf_op jit(solution)/shard_map/all_to_all | solution.py:201
  395.0 1.3 copy-start
where the time goes:
time: 401 us; the launch traced here: 400 us
  Pallas kernels  385 us (96%)
  local copies, waits for them, and re-layouts  9.82 us (2%)
    pallas_call x1, Pallas kernels, by_kernel(): pl.pallas_call(functools.partial(exchange, n, groups), name='exchange', o...  355 us
    pallas_call x1, Pallas kernels, by_kernel(): pl.pallas_call(spread, name='spread', grid=(experts - 1,), out_shape=fina...  26.5 us
  transfers between devices with their start and end apart: 1, of which 0 were waited for; matrix products, arithmetic and copies ran while one was open for 2% of the time, Pallas kernels for 7%

commit v1 on v0

v1 whole, which is shorter than its diff:
```python
import functools

import jax
import jax.numpy as jnp
from jax import lax
from jax.experimental import pallas as pl
from jax.experimental.pallas import tpu as pltpu
from jax.sharding import PartitionSpec as P

MESH = pl.DeviceIdType.MESH
LANES = 128
TAIL = 2
RAMP = 3
AHEAD = 3
SLOTS = 5


def shift(shard, d, f, chips):
    return 2 * ((shard // 2 + d) % chips) + (shard % 2 + f) % 2


def exchange(n, groups, gate, up, router, gain, *refs):
    chips = n // 2
    away = [(d, f) for d in range(1, chips) for f in (0, 1)]
    narrow, near, *far = refs[: 2 + len(away)]
    (
        scale_gate, scale_up, routers, held, out, part, passed, mine, beside, whole, cross, full,
        direct, load_sem, near_send, near_recv, cross_send, cross_recv, full_send, full_recv,
        direct_send, direct_recv, send_sem, recv_sem, keep_sem, tail_recv, pass_send, pass_recv,
        rt_send, rt_recv, rt_keep,
    ) = refs[2 + len(away) :]
    me, group = lax.axis_index("shard"), lax.axis_index("expert")
    core = lax.rem(me, 2)
    items, rows, width, depth = 2 * gate.shape[0], gate.shape[1], out.shape[3], held.shape[0]
    blocks, per, half = gate.shape[2] // LANES, width // LANES, gate.shape[2] // LANES // 2
    share, tokens = part.shape
    last = items - near.shape[0]
    column = [(f, g) for g in range(groups) for f in (0, 1) if (f, g) != (0, 0)]

    def peer(d, f):
        return 2 * lax.rem(me // 2 + d, chips) + lax.rem(core + f, 2)

    def device(d, f, g=0):
        return {"shard": peer(d, f), "expert": lax.rem(group + g, groups)}

    def remote(src, dst, send, recv, to):
        return pltpu.make_async_remote_copy(
            src, dst, send, recv, device_id=to, device_id_type=MESH
        )

    def await_bytes(ref, sem):
        pltpu.make_async_copy(ref, ref, sem).wait()

    def load(k):
        slot, expert = lax.rem(k, depth), k // 2

        @pl.when(lax.rem(k, 2) == 0)
        def _():
            pltpu.make_async_copy(gate.at[expert], held.at[slot], load_sem.at[slot]).start()

        @pl.when(lax.rem(k, 2) == 1)
        def _():
            pltpu.make_async_copy(up.at[expert], held.at[slot], load_sem.at[slot]).start()

    def local(k):
        slot = lax.rem(k, depth)
        await_bytes(held.at[slot], load_sem.at[slot])
        for b in range(blocks):
            values = held[slot, :, b * LANES : (b + 1) * LANES]
            mine[k, b // half, b % half : b % half + 1, :] = jnp.max(
                jnp.abs(values), axis=0, keepdims=True
            )

    def tell(k):
        remote(mine.at[k], beside.at[k], near_send, near_recv.at[k], device(0, 1)).start()

    def ask(k):
        await_bytes(beside.at[k], near_recv.at[k])
        whole[k] = jnp.maximum(mine[k], beside[k])
        for d in range(1, chips):
            remote(
                whole.at[k, core], cross.at[k, d - 1], cross_send, cross_recv.at[k], device(d, 0)
            ).start()

    def relay(k):
        await_bytes(cross.at[k], cross_recv.at[k])
        most = whole[k, core]
        for d in range(1, chips):
            most = jnp.maximum(most, cross[k, d - 1])
        full[k, core] = most
        remote(full.at[k, core], full.at[k, core], full_send, full_recv.at[k], device(0, 1)).start()

    def place(k):
        return narrow.at[lax.rem(k, 2), k // 2, pl.ds(pl.multiple_of(me * rows, rows), rows)]

    def send(k):
        slot = lax.rem(k, SLOTS)
        for d, f in away + [(0, 1)]:
            remote(
                out.at[slot, peer(d, f)], place(k), send_sem.at[slot],
                recv_sem.at[2 * d + f - 1], device(d, f),
            ).start()
        pltpu.make_async_copy(out.at[slot, me], place(k), keep_sem.at[slot]).start()

    def sent(k):
        slot = lax.rem(k, SLOTS)
        await_bytes(out.at[slot, pl.ds(0, n - 1)], send_sem.at[slot])
        await_bytes(out.at[slot, 0], keep_sem.at[slot])

    def leave(k):
        slot, i = lax.rem(k, SLOTS), k - last
        remote(
            out.at[slot, peer(0, 1)], near.at[i, core], send_sem.at[slot], tail_recv, device(0, 1)
        ).start()
        pltpu.make_async_copy(out.at[slot, me], near.at[i, core], keep_sem.at[slot]).start()
        for (d, f), ref in zip(away, far):
            pltpu.make_async_copy(out.at[slot, peer(d, f)], ref.at[i], keep_sem.at[slot]).start()

    def left(k):
        slot = lax.rem(k, SLOTS)
        await_bytes(out.at[slot, 0], send_sem.at[slot])
        await_bytes(out.at[slot, pl.ds(0, n - 1)], keep_sem.at[slot])

    def home(shard):
        return routers.at[
            pl.ds(pl.multiple_of(group * share, share), share),
            pl.ds(pl.multiple_of(shard * tokens, tokens), tokens),
        ]

    def spread_router(block, shard):
        for i, (f, g) in enumerate(column):
            remote(block, home(shard), rt_send.at[i], rt_recv.at[i], device(0, f, g)).start()
        pltpu.make_async_copy(block, home(shard), rt_keep).start()

    for k in range(AHEAD):
        load(jnp.int32(k))
    barrier = pltpu.get_barrier_semaphore()
    for to in [device(d, f) for d, f in away] + [device(0, f, g) for f, g in column]:
        pl.semaphore_signal(barrier, inc=1, device_id=to, device_id_type=MESH)
    part[...] = (router[...] * gain[...]).astype(jnp.bfloat16)
    local(0)
    load(jnp.int32(AHEAD))
    pl.semaphore_wait(barrier, len(away) + len(column))
    for j, (d, f) in enumerate(away + [(0, 1)]):
        remote(mine.at[0], direct.at[j], direct_send, direct_recv, device(d, f)).start()
    for d in range(1, chips):
        remote(part, passed.at[d - 1], pass_send, pass_recv, device(d, 0)).start()
    spread_router(part, me)
    local(1)
    load(jnp.int32(AHEAD + 1))
    tell(1)
    ask(1)
    await_bytes(direct, direct_recv)
    most = mine[0]
    for j in range(n - 1):
        most = jnp.maximum(most, direct[j])
    full[0] = most

    def step(q, _):
        @pl.when(q > 0)
        def _():
            await_bytes(full.at[q, 0], full_recv.at[q])

        @pl.when(q >= SLOTS)
        def _():
            sent(q - SLOTS)

        slot, source = lax.rem(q, SLOTS), lax.rem(q, depth)
        for b in range(blocks):
            at = (b % per) * LANES
            values = held[source, :, b * LANES : (b + 1) * LANES]
            scale = full[q, b // half, b % half : b % half + 1, :]
            out[slot, b // per, :, at : at + LANES] = (values / scale).astype(jnp.bfloat16)

        @pl.when(q < last)
        def _():
            send(q)

        @pl.when(q >= last)
        def _():
            leave(q)

        first = q + jnp.minimum(q, RAMP) + 2
        leads = [(first, first < items), (first + 1, q < RAMP)]
        for k, due in leads:
            @pl.when(due)
            def _():
                local(k)
                tell(k)

                @pl.when(k + AHEAD < items)
                def _():
                    load(k + AHEAD)

        for k, due in leads:
            @pl.when(due)
            def _():
                ask(k)

        @pl.when(q + 1 < items)
        def _():
            relay(q + 1)

        @pl.when(q == RAMP)
        def _():
            await_bytes(passed, pass_recv)
            for d in range(1, chips):
                spread_router(passed.at[d - 1], peer(chips - d, 0))

        return 0

    lax.fori_loop(0, items, step, 0)

    for e in range(items // 2):
        for which, ref in enumerate((scale_gate, scale_up)):
            for i in range(per):
                b = me * per + i
                ref[e : e + 1, i * LANES : (i + 1) * LANES] = full[
                    2 * e + which, b // half, pl.ds(lax.rem(b, half), 1), :
                ]

    def drain(k, _):
        sent(k)
        return 0

    lax.fori_loop(items - SLOTS, last, drain, 0)

    def drain_tail(k, _):
        left(k)
        return 0

    lax.fori_loop(last, items, drain_tail, 0)
    await_bytes(beside.at[pl.ds(1, items - 1)], near_send)
    await_bytes(cross.at[pl.ds(1, items - 1)], cross_send)
    await_bytes(full.at[pl.ds(1, items - 1), 0], full_send)
    await_bytes(direct, direct_send)
    await_bytes(passed, pass_send)
    strip = routers.at[pl.ds(0, share), pl.ds(0, chips * tokens)]
    for i in range(len(column)):
        await_bytes(strip, rt_send.at[i])
        await_bytes(strip, rt_recv.at[i])
    await_bytes(strip, rt_keep)
    await_bytes(near.at[:, 0], tail_recv)
    for j in range(n - 1):
        await_bytes(narrow.at[:, :, pl.ds(0, rows)], recv_sem.at[j])


def spread(narrow, gate, up):
    gate[...] = narrow[0]
    up[...] = narrow[1]


def finish(n, pieces, extras, *refs):
    count = len(pieces)
    arrived, small, results, sems = (
        refs[:count], refs[count : count + extras], refs[count + extras + 2 : -1], refs[-1]
    )
    gate, up, *copies = results
    me, chips = lax.axis_index("shard"), n // 2
    experts, tail, rows = gate.shape[0], arrived[0].shape[0], gate.shape[1] // n
    for at, (piece, ref) in enumerate(zip(pieces, arrived)):
        for i in range(tail):
            final = (gate, up)[i % 2].at[experts - tail // 2 + i // 2]
            for c in range(ref.shape[1]):
                if piece is None:
                    source = 2 * (me // 2) + c
                else:
                    d, f = piece
                    source = 2 * lax.rem(me // 2 + chips - d, chips) + lax.rem(me % 2 + f, 2)
                to = final.at[pl.ds(pl.multiple_of(source * rows, rows), rows)]
                pltpu.make_async_copy(ref.at[i, c], to, sems.at[at]).start()
    for ref, copy in zip(small, copies):
        copy[...] = ref[...]
    for at, ref in enumerate(arrived):
        pltpu.make_async_copy(ref, ref, sems.at[at]).wait()


def by_kernel(n, groups, gate, up, router, gain):
    experts, rows, columns = gate.shape
    width, items, depth, chips = columns // n, 2 * experts, RAMP + AHEAD + 2, n // 2
    tokens, share = router.shape
    half = columns // LANES // 2
    away = [(d, f) for d in range(1, chips) for f in (0, 1)]
    column = 2 * groups - 1
    anywhere = pl.BlockSpec(memory_space=pl.ANY)
    inside = pl.BlockSpec(memory_space=pltpu.VMEM)
    dma = pltpu.SemaphoreType.DMA
    bf16 = functools.partial(jax.ShapeDtypeStruct, dtype=jnp.bfloat16)
    maxima = pltpu.VMEM((items, 2, half, LANES), jnp.float32)
    narrow, near, *far, scale_gate, scale_up, routers = pl.pallas_call(
        functools.partial(exchange, n, groups),
        name="exchange",
        out_shape=(
            bf16((2, experts - TAIL, n * rows, width)),
            bf16((2 * TAIL, 2, rows, width)),
            *[bf16((2 * TAIL, rows, width)) for _ in away],
            jax.ShapeDtypeStruct((experts, width), jnp.float32),
            jax.ShapeDtypeStruct((experts, width), jnp.float32),
            bf16((groups * share, n * tokens)),
        ),
        in_specs=[anywhere, anywhere, inside, inside],
        out_specs=(anywhere,) * (2 + len(away)) + (inside, inside, anywhere),
        scratch_shapes=[
            pltpu.VMEM((depth, rows, columns), jnp.float32),
            pltpu.VMEM((SLOTS, n, rows, width), jnp.bfloat16),
            pltpu.VMEM((share, tokens), jnp.bfloat16),
            pltpu.VMEM((chips - 1, share, tokens), jnp.bfloat16),
            maxima,
            maxima,
            maxima,
            pltpu.VMEM((items, chips - 1, half, LANES), jnp.float32),
            maxima,
            pltpu.VMEM((n - 1, 2, half, LANES), jnp.float32),
            dma((depth,)),
            dma,
            dma((items,)),
            dma,
            dma((items,)),
            dma,
            dma((items,)),
            dma,
            dma,
            dma((SLOTS,)),
            dma((n - 1,)),
            dma((SLOTS,)),
            dma,
            dma,
            dma,
            dma((column,)),
            dma((column,)),
            dma,
        ],
        compiler_params=pltpu.CompilerParams(collective_id=0, has_side_effects=True),
    )(gate, up, router.T, gain.reshape(1, tokens))
    arrived = [
        lax.ppermute(ref, "shard", [(s, shift(s, d, f, chips)) for s in range(n)])
        for (d, f), ref in zip(away, far)
    ]
    finals = (bf16((experts, n * rows, width)),) * 2
    final = pl.pallas_call(
        spread,
        name="spread",
        grid=(experts - TAIL,),
        out_shape=finals,
        in_specs=[pl.BlockSpec((2, 1, n * rows, width), lambda e: (0, e, 0, 0))],
        out_specs=(pl.BlockSpec((1, n * rows, width), lambda e: (e, 0, 0)),) * 2,
        cost_estimate=pl.CostEstimate(flops=0, bytes_accessed=4 * narrow.size, transcendentals=0),
    )(narrow)

    def put(name, pieces, blocks, final, small=()):
        count = len(blocks) + len(small)
        return pl.pallas_call(
            functools.partial(finish, n, pieces, len(small)),
            name=name,
            out_shape=finals + tuple(jax.ShapeDtypeStruct(s.shape, s.dtype) for s in small),
            in_specs=[inside] * count + [anywhere] * 2,
            out_specs=(anywhere,) * 2 + (inside,) * len(small),
            scratch_shapes=[dma((len(blocks),))],
            input_output_aliases={count: 0, count + 1: 1},
            compiler_params=pltpu.CompilerParams(vmem_limit_bytes=16 * 2**20),
        )(*blocks, *small, *final)

    blocks = [jnp.expand_dims(ref, 1) for ref in arrived]
    *final, scale_gate, scale_up, routers = put(
        "finish_near", [None] + away[:-1], [near] + blocks[:-1], final,
        (scale_gate, scale_up, routers),
    )
    final_gate, final_up = put("finish_far", away[-1:], blocks[-1:], final)
    return final_gate, final_up, scale_gate, scale_up, routers.T


def by_collectives(gate, up, router, gain):
    scale_gate, scale_up = lax.pmax(
        (jnp.max(jnp.abs(gate), axis=1), jnp.max(jnp.abs(up), axis=1)), "shard"
    )

    def serve(master, scale):
        narrow = (master / jnp.expand_dims(scale, 1)).astype(jnp.bfloat16)
        final = lax.all_to_all(narrow, "shard", split_axis=2, concat_axis=1, tiled=True)
        width = final.shape[2]
        return final, lax.dynamic_slice_in_dim(
            scale, lax.axis_index("shard") * width, width, axis=1
        )

    final_gate, scale_gate = serve(gate, scale_gate)
    final_up, scale_up = serve(up, scale_up)
    part = (router * gain[:, None]).astype(jnp.bfloat16)
    rows = lax.all_gather(part, "shard", axis=0, tiled=True)
    return final_gate, final_up, scale_gate, scale_up, lax.all_gather(rows, "expert", axis=1, tiled=True)


def solution(mesh):
    n, groups = mesh.shape["shard"], mesh.shape["expert"]

    def shards(gate, up, router, gain):
        aligned = gate.shape[2] % (n * LANES) == 0 and gate.shape[1] % 16 == 0
        aligned = aligned and gate.shape[0] > TAIL + SLOTS + RAMP and 2 * TAIL <= SLOTS
        aligned = aligned and router.shape[0] % LANES == 0 and router.shape[1] % 16 == 0
        if n >= 4 and n % 2 == 0 and aligned:
            return by_kernel(n, groups, gate, up, router, gain)
        return by_collectives(gate, up, router, gain)

    return jax.shard_map(
        shards,
        mesh=mesh,
        in_specs=(
            P(("shift", "expert"), "shard", None),
            P(("shift", "expert"), "shard", None),
            P(("shift", "shard"), "expert"),
            P(("shift", "shard")),
        ),
        out_specs=(
            P(("shift", "expert"), None, "shard"),
            P(("shift", "expert"), None, "shard"),
            P(("shift", "expert"), "shard"),
            P(("shift", "expert"), "shard"),
            P("shift", None),
        ),
        check_vma=False,
    )
```

time: 401 us -> 378 us (0.943)
  Pallas kernels: 385 us -> 356 us
  waiting for transfers between devices: 0.01 us -> 18.1 us
  local copies, waits for them, and re-layouts: 9.82 us -> 0.02 us
    pallas_call x1, Pallas kernels: 355 us -> 328 us  [by_kernel(): pl.pallas_call(functools.partial(exchange, n, groups), name='exchange', o...]
    ppermute x0 -> x2, waiting for transfers between devices: none -> 18.1 us  [by_kernel(): lax.ppermute(ref, 'shard', [(s, shift(s, d, f, chips)) for s in range(n)])]
    reshape x3 -> x0, local copies, waits for them, and re-layouts: 5.12 us -> none  [the longest x1 3.41 us: by_kernel(): serve_router = routers.reshape(groups, n * tokens, share).transpose(1, 0, 2)]
    pallas_call x2 -> x3, Pallas kernels: 30.3 us -> 28.5 us  [the longest x1 23.9 us: by_kernel(): pl.pallas_call(spread, name='spread', grid=(experts - TAIL,), out_shape=f...]
  transfers between devices with their start and end apart: 1 -> 2, of which waited for: 0 -> 1; matrix products, arithmetic and copies ran while one was open for 2% -> 0% of each run, Pallas kernels for 7% -> 7%
where the time goes in v1:
time: 378 us; the launch traced here: 377 us
  Pallas kernels  356 us (94%)
  waiting for transfers between devices  18.1 us (5%)
    pallas_call x1, Pallas kernels, by_kernel(): pl.pallas_call(functools.partial(exchange, n, groups), name='exchange', o...  328 us
    pallas_call x1, Pallas kernels, by_kernel(): pl.pallas_call(spread, name='spread', grid=(experts - TAIL,), out_shape=f...  23.9 us
    ppermute x2, waiting for transfers between devices, by_kernel(): lax.ppermute(ref, 'shard', [(s, shift(s, d, f, chips)) for s in range(n)])  18.1 us
  transfers between devices with their start and end apart: 2, of which 1 were waited for; matrix products, arithmetic and copies ran while one was open for 0% of the time, Pallas kernels for 7%

profile of v1, /device:TPU:1, one launch (start us, length us, event | category | flops | bytes accessed | tf_op | source)
XLA Modules:
  0.0 377.3 jit_solution(2444348033878283620)
XLA Ops:
  0.6 328.0 %exchange.1 = (bf16[2,14,2048,256]{3,2,1,0:T(8,128)(2,1)}, bf16[4,2,512,256]{3,2,1,0:T(8,128)(2,1)}, bf16[4,512,256]{2,1,0:T(8,128)(2,1)}, bf16[4,512,256]{2,1,0...) custom-call(f32[16,512,1024]{2,1,0:T(8,128)} %gate.1, f32[16,512,1024]{2,1,0:T(8,128)} %up.1, ...), custom_call_target="tpu_custom_call" | custom-call | tf_op jit(solution)/shard_map/exchange/pallas_call | solution.py:290
  328.6 0.0 copy-start
  328.6 0.0 copy-start.1
  328.7 0.0 copy-start.2
  328.7 0.0 copy-start.3
  328.7 1.3 collective-permute-start.1
  330.0 0.7 collective-permute-start
  330.6 23.9 %spread.1 = (bf16[16,2048,256]{2,1,0:T(8,128)(2,1)}, bf16[16,2048,256]{2,1,0:T(8,128)(2,1)}) custom-call(bf16[2,14,2048,256]{3,2,1,0:T(8,128)(2,1)} %get-tuple-element.27.narrow), custom_call_target="tpu_custom_call" | custom-call | bytes 58720256 | tf_op jit(solution)/shard_map/spread/pallas_call | solution.py:340
  354.5 0.0 collective-permute-done.1
  354.5 0.0 copy-done
  354.5 0.0 copy-done.1
  354.5 0.0 copy-done.2
  354.5 0.0 copy-done.3
  354.5 3.6 finish_near.1
  358.2 18.1 %collective-permute-done = bf16[4,512,256]{2,1,0:T(8,128)(2,1)S(1)} collective-permute-done((bf16[4,512,256]{2,1,0:T(8,128)(2,1)}, bf16[4,512,256]{2,1,0:T(8,128)(2,1)S(1)}, u32[]{:S(2)}, u32[]{:S(2)}) %collective-permute-start) | collective-permute-done | bytes 1048608 | tf_op jit(solution)/shard_map/ppermute | solution.py:336
  376.3 1.0 finish_far.1
Async XLA Ops:
  328.6 25.9 %copy-start = (bf16[4,2,512,256]{3,2,1,0:T(8,128)(2,1)S(1)}, bf16[4,2,512,256]{3,2,1,0:T(8,128)(2,1)}, u32[]{:S(2)}) copy-start(bf16[4,2,512,256]{3,2,1,0:T(8,128)(2,1)} %get-tuple-element.22.refs_0_) | copy-start | bytes 6291460
  328.6 25.9 %copy-start.1 = (bf16[64,2048]{1,0:T(8,128)(2,1)S(1)}, bf16[64,2048]{1,0:T(8,128)(2,1)}, u32[]{:S(2)}) copy-start(bf16[64,2048]{1,0:T(8,128)(2,1)} %get-tuple-element.26.refs_4_) | copy-start | bytes 786436
  328.7 25.9 %copy-start.2 = (f32[16,256]{1,0:T(8,128)S(1)}, f32[16,256]{1,0:T(8,128)}, u32[]{:S(2)}) copy-start(f32[16,256]{1,0:T(8,128)} %get-tuple-element.24.refs_2_) | copy-start | bytes 49156
  328.7 25.9 %copy-start.3 = (f32[16,256]{1,0:T(8,128)S(1)}, f32[16,256]{1,0:T(8,128)}, u32[]{:S(2)}) copy-start(f32[16,256]{1,0:T(8,128)} %get-tuple-element.25.refs_3_) | copy-start | bytes 49156
  328.7 25.8 %collective-permute-start.1 = (bf16[4,512,256]{2,1,0:T(8,128)(2,1)}, bf16[4,512,256]{2,1,0:T(8,128)(2,1)}, u32[]{:S(2)}, u32[]{:S(2)}) collective-permute-start(bf16[4,512,256]{2,1,0:T(8,128)(2,1)} %get-tuple-element.23), channel_id=1, source_target_pairs={{0,2},{1,3},{2,0},{3,1},{4,6},{5,7},{6,4},{7,5},{8,10},{9,11},{10,... | collective-permute-start | bytes 3145736 | tf_op jit(solution)/shard_map/ppermute | solution.py:336
  330.0 46.4 %collective-permute-start = (bf16[4,512,256]{2,1,0:T(8,128)(2,1)}, bf16[4,512,256]{2,1,0:T(8,128)(2,1)S(1)}, u32[]{:S(2)}, u32[]{:S(2)}) collective-permute-start(bf16[4,512,256]{2,1,0:T(8,128)(2,1)} %get-tuple-element.21), channel_id=1, source_target_pairs={{0,3},{1,2},{2,1},{3,0},{4,7},{5,6},{6,5},{7,4},{8,11},{9,10},{10,... | collective-permute-start | bytes 3145736 | tf_op jit(solution)/shard_map/ppermute | solution.py:336

commit v2 on v1

--- a/solution.py
+++ b/solution.py
@@ -12,7 +12,7 @@
 TAIL = 2
 RAMP = 3
 AHEAD = 3
-SLOTS = 5
+SLOTS = 6
 
 
 def shift(shard, d, f, chips):
@@ -22,12 +22,13 @@
 def exchange(n, groups, gate, up, router, gain, *refs):
     chips = n // 2
     away = [(d, f) for d in range(1, chips) for f in (0, 1)]
+    same, other = [p for p in away if p[1] == 0], [p for p in away if p[1] == 1]
     narrow, near, *far = refs[: 2 + len(away)]
     (
         scale_gate, scale_up, routers, held, out, part, passed, mine, beside, whole, cross, full,
         direct, load_sem, near_send, near_recv, cross_send, cross_recv, full_send, full_recv,
         direct_send, direct_recv, send_sem, recv_sem, keep_sem, tail_recv, pass_send, pass_recv,
-        rt_send, rt_recv, rt_keep,
+        rt_send, rt_recv, rt_keep, go,
     ) = refs[2 + len(away) :]
     me, group = lax.axis_index("shard"), lax.axis_index("expert")
     core = lax.rem(me, 2)
@@ -93,13 +94,17 @@
     def place(k):
         return narrow.at[lax.rem(k, 2), k // 2, pl.ds(pl.multiple_of(me * rows, rows), rows)]
 
-    def send(k):
+    def send(k, pieces):
         slot = lax.rem(k, SLOTS)
-        for d, f in away + [(0, 1)]:
+        for d, f in pieces:
             remote(
                 out.at[slot, peer(d, f)], place(k), send_sem.at[slot],
                 recv_sem.at[2 * d + f - 1], device(d, f),
             ).start()
+
+    def keep(k):
+        slot = lax.rem(k, SLOTS)
+        send(k, [(0, 1)])
         pltpu.make_async_copy(out.at[slot, me], place(k), keep_sem.at[slot]).start()
 
     def sent(k):
@@ -161,7 +166,7 @@
         def _():
             await_bytes(full.at[q, 0], full_recv.at[q])
 
-        @pl.when(q >= SLOTS)
+        @pl.when((q > SLOTS) | ((q == SLOTS) & (core == 1)))
         def _():
             sent(q - SLOTS)
 
@@ -172,9 +177,13 @@
             scale = full[q, b // half, b % half : b % half + 1, :]
             out[slot, b // per, :, at : at + LANES] = (values / scale).astype(jnp.bfloat16)
 
+        @pl.when((q < last) & (core == 0))
+        def _():
+            send(q, same + other)
+
         @pl.when(q < last)
         def _():
-            send(q)
+            keep(q)
 
         @pl.when(q >= last)
         def _():
@@ -200,6 +209,24 @@
         @pl.when(q + 1 < items)
         def _():
             relay(q + 1)
+
+        @pl.when((q == 1) & (core == 0))
+        def _():
+            sent(0)
+            pl.semaphore_signal(go, inc=1, device_id=device(0, 1), device_id_type=MESH)
+
+        @pl.when((q == 1) & (core == 1))
+        def _():
+            pl.semaphore_wait(go, 1)
+            send(0, other)
+
+        @pl.when((q > 0) & (q < last) & (core == 1))
+        def _():
+            send(q, other)
+
+        @pl.when((q > 0) & (q <= last) & (core == 1))
+        def _():
+            send(q - 1, same)
 
         @pl.when(q == RAMP)
         def _():
@@ -329,6 +356,7 @@
             dma((column,)),
             dma((column,)),
             dma,
+            pltpu.SemaphoreType.REGULAR,
         ],
         compiler_params=pltpu.CompilerParams(collective_id=0, has_side_effects=True),
     )(gate, up, router.T, gain.reshape(1, tokens))

time: 378 us -> 374 us (0.989)
  waiting for transfers between devices: 18.1 us -> 13.8 us
    ppermute x2, waiting for transfers between devices: 18.1 us -> 13.8 us  [by_kernel(): lax.ppermute(ref, 'shard', [(s, shift(s, d, f, chips)) for s in range(n)])]
  transfers between devices with their start and end apart: 2 -> 2, of which waited for: 1 -> 2; matrix products, arithmetic and copies ran while one was open for 0% -> 0% of each run, Pallas kernels for 7% -> 7%
where the time goes in v2:
time: 374 us; the launch traced here: 373 us
  Pallas kernels  357 us (95%)
  waiting for transfers between devices  13.8 us (4%)
    pallas_call x1, Pallas kernels, by_kernel(): pl.pallas_call(functools.partial(exchange, n, groups), name='exchange', o...  328 us
    pallas_call x1, Pallas kernels, by_kernel(): pl.pallas_call(spread, name='spread', grid=(experts - TAIL,), out_shape=f...  23.9 us
    ppermute x2, waiting for transfers between devices, by_kernel(): lax.ppermute(ref, 'shard', [(s, shift(s, d, f, chips)) for s in range(n)])  13.8 us
  transfers between devices with their start and end apart: 2, of which 2 were waited for; matrix products, arithmetic and copies ran while one was open for 0% of the time, Pallas kernels for 7%

profile of v2, /device:TPU:1, one launch (start us, length us, event | category | flops | bytes accessed | tf_op | source)
XLA Modules:
  0.0 372.7 jit_solution(15068597710288663532)
XLA Ops:
  0.6 328.5 %exchange.1 = (bf16[2,14,2048,256]{3,2,1,0:T(8,128)(2,1)}, bf16[4,2,512,256]{3,2,1,0:T(8,128)(2,1)}, bf16[4,512,256]{2,1,0:T(8,128)(2,1)}, bf16[4,512,256]{2,1,0...) custom-call(f32[16,512,1024]{2,1,0:T(8,128)} %gate.1, f32[16,512,1024]{2,1,0:T(8,128)} %up.1, ...), custom_call_target="tpu_custom_call" | custom-call | tf_op jit(solution)/shard_map/exchange/pallas_call | solution.py:317
  329.1 0.0 copy-start
  329.1 0.0 copy-start.1
  329.1 0.0 copy-start.2
  329.1 0.0 copy-start.3
  329.1 1.3 collective-permute-start.1
  330.4 0.0 collective-permute-start
  330.4 23.9 %spread.1 = (bf16[16,2048,256]{2,1,0:T(8,128)(2,1)}, bf16[16,2048,256]{2,1,0:T(8,128)(2,1)}) custom-call(bf16[2,14,2048,256]{3,2,1,0:T(8,128)(2,1)} %get-tuple-element.27.narrow), custom_call_target="tpu_custom_call" | custom-call | bytes 58720256 | tf_op jit(solution)/shard_map/spread/pallas_call | solution.py:368
  354.3 0.1 collective-permute-done.1
  354.4 0.0 copy-done
  354.4 0.0 copy-done.1
  354.4 0.0 copy-done.2
  354.4 0.0 copy-done.3
  354.4 3.6 finish_near.1
  358.0 13.7 %collective-permute-done = bf16[4,512,256]{2,1,0:T(8,128)(2,1)S(1)} collective-permute-done((bf16[4,512,256]{2,1,0:T(8,128)(2,1)}, bf16[4,512,256]{2,1,0:T(8,128)(2,1)S(1)}, u32[]{:S(2)}, u32[]{:S(2)}) %collective-permute-start) | collective-permute-done | bytes 1048608 | tf_op jit(solution)/shard_map/ppermute | solution.py:364
  371.7 1.0 finish_far.1
Async XLA Ops:
  329.1 25.3 %copy-start = (bf16[4,2,512,256]{3,2,1,0:T(8,128)(2,1)S(1)}, bf16[4,2,512,256]{3,2,1,0:T(8,128)(2,1)}, u32[]{:S(2)}) copy-start(bf16[4,2,512,256]{3,2,1,0:T(8,128)(2,1)} %get-tuple-element.22.refs_0_) | copy-start | bytes 6291460
  329.1 25.3 %copy-start.1 = (bf16[64,2048]{1,0:T(8,128)(2,1)S(1)}, bf16[64,2048]{1,0:T(8,128)(2,1)}, u32[]{:S(2)}) copy-start(bf16[64,2048]{1,0:T(8,128)(2,1)} %get-tuple-element.26.refs_4_) | copy-start | bytes 786436
  329.1 25.3 %copy-start.2 = (f32[16,256]{1,0:T(8,128)S(1)}, f32[16,256]{1,0:T(8,128)}, u32[]{:S(2)}) copy-start(f32[16,256]{1,0:T(8,128)} %get-tuple-element.24.refs_2_) | copy-start | bytes 49156
  329.1 25.3 %copy-start.3 = (f32[16,256]{1,0:T(8,128)S(1)}, f32[16,256]{1,0:T(8,128)}, u32[]{:S(2)}) copy-start(f32[16,256]{1,0:T(8,128)} %get-tuple-element.25.refs_3_) | copy-start | bytes 49156
  329.1 25.3 %collective-permute-start.1 = (bf16[4,512,256]{2,1,0:T(8,128)(2,1)}, bf16[4,512,256]{2,1,0:T(8,128)(2,1)}, u32[]{:S(2)}, u32[]{:S(2)}) collective-permute-start(bf16[4,512,256]{2,1,0:T(8,128)(2,1)} %get-tuple-element.23), channel_id=1, source_target_pairs={{0,2},{1,3},{2,0},{3,1},{4,6},{5,7},{6,4},{7,5},{8,10},{9,11},{10,... | collective-permute-start | bytes 3145736 | tf_op jit(solution)/shard_map/ppermute | solution.py:364
  330.4 41.3 %collective-permute-start = (bf16[4,512,256]{2,1,0:T(8,128)(2,1)}, bf16[4,512,256]{2,1,0:T(8,128)(2,1)S(1)}, u32[]{:S(2)}, u32[]{:S(2)}) collective-permute-start(bf16[4,512,256]{2,1,0:T(8,128)(2,1)} %get-tuple-element.21), channel_id=1, source_target_pairs={{0,3},{1,2},{2,1},{3,0},{4,7},{5,6},{6,5},{7,4},{8,11},{9,10},{10,... | collective-permute-start | bytes 3145736 | tf_op jit(solution)/shard_map/ppermute | solution.py:364

commit v3 on v2

--- a/solution.py
+++ b/solution.py
@@ -13,36 +13,35 @@
 RAMP = 3
 AHEAD = 3
 SLOTS = 6
+CHUNKS = 4
 
 
 def shift(shard, d, f, chips):
     return 2 * ((shard // 2 + d) % chips) + (shard % 2 + f) % 2
 
 
-def exchange(n, groups, gate, up, router, gain, *refs):
+def exchange(n, gate, up, router, gain, *refs):
     chips = n // 2
     away = [(d, f) for d in range(1, chips) for f in (0, 1)]
     same, other = [p for p in away if p[1] == 0], [p for p in away if p[1] == 1]
     narrow, near, *far = refs[: 2 + len(away)]
     (
-        scale_gate, scale_up, routers, held, out, part, passed, mine, beside, whole, cross, full,
-        direct, load_sem, near_send, near_recv, cross_send, cross_recv, full_send, full_recv,
-        direct_send, direct_recv, send_sem, recv_sem, keep_sem, tail_recv, pass_send, pass_recv,
-        rt_send, rt_recv, rt_keep, go,
+        scale_gate, scale_up, pair, held, out, weight, by, part, scales, mine, beside, whole, cross,
+        full, direct, first_sem, load_sem, near_send, near_recv, cross_send, cross_recv, full_send,
+        full_recv, direct_send, direct_recv, send_sem, recv_sem, keep_sem, tail_recv, small_sem,
+        pass_send, pass_recv, scale_sem, go,
     ) = refs[2 + len(away) :]
-    me, group = lax.axis_index("shard"), lax.axis_index("expert")
+    me = lax.axis_index("shard")
     core = lax.rem(me, 2)
     items, rows, width, depth = 2 * gate.shape[0], gate.shape[1], out.shape[3], held.shape[0]
     blocks, per, half = gate.shape[2] // LANES, width // LANES, gate.shape[2] // LANES // 2
-    share, tokens = part.shape
-    last = items - near.shape[0]
-    column = [(f, g) for g in range(groups) for f in (0, 1) if (f, g) != (0, 0)]
+    last, chunk = items - near.shape[0], rows // CHUNKS
 
     def peer(d, f):
         return 2 * lax.rem(me // 2 + d, chips) + lax.rem(core + f, 2)
 
-    def device(d, f, g=0):
-        return {"shard": peer(d, f), "expert": lax.rem(group + g, groups)}
+    def device(d, f):
+        return {"shard": peer(d, f)}
 
     def remote(src, dst, send, recv, to):
         return pltpu.make_async_remote_copy(
@@ -62,6 +61,10 @@
         @pl.when(lax.rem(k, 2) == 1)
         def _():
             pltpu.make_async_copy(up.at[expert], held.at[slot], load_sem.at[slot]).start()
+
+    def first(c):
+        at = pl.ds(c * chunk, chunk)
+        return pltpu.make_async_copy(gate.at[0, at], held.at[0, at], first_sem.at[c])
 
     def local(k):
         slot = lax.rem(k, depth)
@@ -72,6 +75,16 @@
                 jnp.abs(values), axis=0, keepdims=True
             )
 
+    def scaled(k, shard):
+        slot, source = lax.rem(k, SLOTS), lax.rem(k, depth)
+        for i in range(per):
+            b = shard * per + i
+            values = held[source, :, pl.ds(pl.multiple_of(b * LANES, LANES), LANES)]
+            scale = full[k, b // half, pl.ds(lax.rem(b, half), 1), :]
+            out[slot, shard, :, i * LANES : (i + 1) * LANES] = (values / scale).astype(
+                jnp.bfloat16
+            )
+
     def tell(k):
         remote(mine.at[k], beside.at[k], near_send, near_recv.at[k], device(0, 1)).start()
 
@@ -126,34 +139,37 @@
         await_bytes(out.at[slot, 0], send_sem.at[slot])
         await_bytes(out.at[slot, pl.ds(0, n - 1)], keep_sem.at[slot])
 
-    def home(shard):
-        return routers.at[
-            pl.ds(pl.multiple_of(group * share, share), share),
-            pl.ds(pl.multiple_of(shard * tokens, tokens), tokens),
-        ]
-
-    def spread_router(block, shard):
-        for i, (f, g) in enumerate(column):
-            remote(block, home(shard), rt_send.at[i], rt_recv.at[i], device(0, f, g)).start()
-        pltpu.make_async_copy(block, home(shard), rt_keep).start()
-
-    for k in range(AHEAD):
+    for c in range(CHUNKS):
+        first(c).start()
+    barrier = pltpu.get_barrier_semaphore()
+    for d, f in away + [(0, 1)]:
+        pl.semaphore_signal(barrier, inc=1, device_id=device(d, f), device_id_type=MESH)
+    small = [
+        pltpu.make_async_copy(router, weight, small_sem.at[0]),
+        pltpu.make_async_copy(gain, by, small_sem.at[1]),
+    ]
+    for c in range(CHUNKS):
+        first(c).wait()
+        if c == 0:
+            load(jnp.int32(1))
+        for b in range(blocks):
+            values = held[0, c * chunk : (c + 1) * chunk, b * LANES : (b + 1) * LANES]
+            most = jnp.max(jnp.abs(values), axis=0, keepdims=True)
+            at = b // half, slice(b % half, b % half + 1)
+            mine[(0, *at)] = most if c == 0 else jnp.maximum(mine[(0, *at)], most)
+    for k in range(2, AHEAD + 1):
         load(jnp.int32(k))
-    barrier = pltpu.get_barrier_semaphore()
-    for to in [device(d, f) for d, f in away] + [device(0, f, g) for f, g in column]:
-        pl.semaphore_signal(barrier, inc=1, device_id=to, device_id_type=MESH)
-    part[...] = (router[...] * gain[...]).astype(jnp.bfloat16)
-    local(0)
-    load(jnp.int32(AHEAD))
-    pl.semaphore_wait(barrier, len(away) + len(column))
+    for copy in small:
+        copy.start()
+    pl.semaphore_wait(barrier, n - 1)
     for j, (d, f) in enumerate(away + [(0, 1)]):
         remote(mine.at[0], direct.at[j], direct_send, direct_recv, device(d, f)).start()
-    for d in range(1, chips):
-        remote(part, passed.at[d - 1], pass_send, pass_recv, device(d, 0)).start()
-    spread_router(part, me)
     local(1)
     load(jnp.int32(AHEAD + 1))
     tell(1)
+    for copy in small:
+        copy.wait()
+    part[...] = (weight[...] * by[...]).astype(jnp.bfloat16)
     ask(1)
     await_bytes(direct, direct_recv)
     most = mine[0]
@@ -170,16 +186,15 @@
         def _():
             sent(q - SLOTS)
 
-        slot, source = lax.rem(q, SLOTS), lax.rem(q, depth)
-        for b in range(blocks):
-            at = (b % per) * LANES
-            values = held[source, :, b * LANES : (b + 1) * LANES]
-            scale = full[q, b // half, b % half : b % half + 1, :]
-            out[slot, b // per, :, at : at + LANES] = (values / scale).astype(jnp.bfloat16)
-
-        @pl.when((q < last) & (core == 0))
-        def _():
-            send(q, same + other)
+        before = None
+        for d, f in away + [(0, 1), (0, 0)]:
+            scaled(q, peer(d, f))
+            if before is not None:
+                @pl.when((q < last) & (core == 0))
+                def _():
+                    send(q, [before])
+
+            before = (d, f) if d > 0 else None
 
         @pl.when(q < last)
         def _():
@@ -230,21 +245,24 @@
 
         @pl.when(q == RAMP)
         def _():
-            await_bytes(passed, pass_recv)
+            pltpu.make_async_copy(part, pair.at[0], small_sem.at[0]).start()
             for d in range(1, chips):
-                spread_router(passed.at[d - 1], peer(chips - d, 0))
+                remote(part, pair.at[d], pass_send, pass_recv, device(d, 0)).start()
 
         return 0
 
     lax.fori_loop(0, items, step, 0)
 
     for e in range(items // 2):
-        for which, ref in enumerate((scale_gate, scale_up)):
+        for which in (0, 1):
             for i in range(per):
                 b = me * per + i
-                ref[e : e + 1, i * LANES : (i + 1) * LANES] = full[
+                scales[which, e : e + 1, i * LANES : (i + 1) * LANES] = full[
                     2 * e + which, b // half, pl.ds(lax.rem(b, half), 1), :
                 ]
+
+    for which, ref in enumerate((scale_gate, scale_up)):
+        pltpu.make_async_copy(scales.at[which], ref, scale_sem.at[which]).start()
 
     def drain(k, _):
         sent(k)
@@ -261,20 +279,53 @@
     await_bytes(cross.at[pl.ds(1, items - 1)], cross_send)
     await_bytes(full.at[pl.ds(1, items - 1), 0], full_send)
     await_bytes(direct, direct_send)
-    await_bytes(passed, pass_send)
-    strip = routers.at[pl.ds(0, share), pl.ds(0, chips * tokens)]
-    for i in range(len(column)):
-        await_bytes(strip, rt_send.at[i])
-        await_bytes(strip, rt_recv.at[i])
-    await_bytes(strip, rt_keep)
+    rest = pair.at[pl.ds(1, chips - 1)]
+    await_bytes(rest, pass_send)
+    await_bytes(rest, pass_recv)
+    await_bytes(part, small_sem.at[0])
+    for which in (0, 1):
+        await_bytes(scales.at[which], scale_sem.at[which])
     await_bytes(near.at[:, 0], tail_recv)
     for j in range(n - 1):
         await_bytes(narrow.at[:, :, pl.ds(0, rows)], recv_sem.at[j])
 
 
-def spread(narrow, gate, up):
+def gather(n, groups, token, pair, routers, send_sem, recv_sem, keep_sem):
+    del token
+    me, group, chips = lax.axis_index("shard"), lax.axis_index("expert"), n // 2
+    core, (_, share, tokens) = lax.rem(me, 2), pair.shape
+    column = [(f, g) for g in range(groups) for f in (0, 1) if (f, g) != (0, 0)]
+
+    def device(f, g):
+        near = me - core + lax.rem(core + f, 2)
+        return {"shard": near, "expert": lax.rem(group + g, groups)}
+
+    barrier = pltpu.get_barrier_semaphore()
+    for f, g in column:
+        pl.semaphore_signal(barrier, inc=1, device_id=device(f, g), device_id_type=MESH)
+    pl.semaphore_wait(barrier, len(column))
+    for d in range(chips):
+        shard = 2 * lax.rem(me // 2 + chips - d, chips) + core
+        home = routers.at[
+            pl.ds(pl.multiple_of(group * share, share), share),
+            pl.ds(pl.multiple_of(shard * tokens, tokens), tokens),
+        ]
+        for i, (f, g) in enumerate(column):
+            pltpu.make_async_remote_copy(
+                pair.at[d], home, send_sem.at[i], recv_sem.at[i],
+                device_id=device(f, g), device_id_type=MESH,
+            ).start()
+        pltpu.make_async_copy(pair.at[d], home, keep_sem).start()
+    for i in range(len(column)):
+        pltpu.make_async_copy(pair, pair, send_sem.at[i]).wait()
+        pltpu.make_async_copy(pair, pair, recv_sem.at[i]).wait()
+    pltpu.make_async_copy(pair, pair, keep_sem).wait()
+
+
+def spread(narrow, gate, up, token):
     gate[...] = narrow[0]
     up[...] = narrow[1]
+    token[...] = jnp.zeros_like(token)
 
 
 def finish(n, pieces, extras, *refs):
@@ -309,35 +360,39 @@
     half = columns // LANES // 2
     away = [(d, f) for d in range(1, chips) for f in (0, 1)]
     column = 2 * groups - 1
+    f32 = functools.partial(jax.ShapeDtypeStruct, dtype=jnp.float32)
     anywhere = pl.BlockSpec(memory_space=pl.ANY)
     inside = pl.BlockSpec(memory_space=pltpu.VMEM)
     dma = pltpu.SemaphoreType.DMA
     bf16 = functools.partial(jax.ShapeDtypeStruct, dtype=jnp.bfloat16)
     maxima = pltpu.VMEM((items, 2, half, LANES), jnp.float32)
-    narrow, near, *far, scale_gate, scale_up, routers = pl.pallas_call(
-        functools.partial(exchange, n, groups),
+    narrow, near, *far, scale_gate, scale_up, pair = pl.pallas_call(
+        functools.partial(exchange, n),
         name="exchange",
         out_shape=(
             bf16((2, experts - TAIL, n * rows, width)),
             bf16((2 * TAIL, 2, rows, width)),
             *[bf16((2 * TAIL, rows, width)) for _ in away],
-            jax.ShapeDtypeStruct((experts, width), jnp.float32),
-            jax.ShapeDtypeStruct((experts, width), jnp.float32),
-            bf16((groups * share, n * tokens)),
+            f32((experts, width)),
+            f32((experts, width)),
+            bf16((chips, share, tokens)),
         ),
-        in_specs=[anywhere, anywhere, inside, inside],
-        out_specs=(anywhere,) * (2 + len(away)) + (inside, inside, anywhere),
+        in_specs=[anywhere] * 4,
+        out_specs=(anywhere,) * (5 + len(away)),
         scratch_shapes=[
             pltpu.VMEM((depth, rows, columns), jnp.float32),
             pltpu.VMEM((SLOTS, n, rows, width), jnp.bfloat16),
+            pltpu.VMEM((share, tokens), jnp.float32),
+            pltpu.VMEM((1, tokens), jnp.float32),
             pltpu.VMEM((share, tokens), jnp.bfloat16),
-            pltpu.VMEM((chips - 1, share, tokens), jnp.bfloat16),
+            pltpu.VMEM((2, experts, width), jnp.float32),
             maxima,
             maxima,
             maxima,
             pltpu.VMEM((items, chips - 1, half, LANES), jnp.float32),
             maxima,
             pltpu.VMEM((n - 1, 2, half, LANES), jnp.float32),
+            dma((CHUNKS,)),
             dma((depth,)),
             dma,
             dma((items,)),
@@ -351,11 +406,10 @@
             dma((n - 1,)),
             dma((SLOTS,)),
             dma,
-            dma,
-            dma,
-            dma((column,)),
-            dma((column,)),
-            dma,
+            dma((2,)),
+            dma,
+            dma,
+            dma((2,)),
             pltpu.SemaphoreType.REGULAR,
         ],
         compiler_params=pltpu.CompilerParams(collective_id=0, has_side_effects=True),
@@ -365,15 +419,28 @@
         for (d, f), ref in zip(away, far)
     ]
     finals = (bf16((experts, n * rows, width)),) * 2
-    final = pl.pallas_call(
+    *final, token = pl.pallas_call(
         spread,
         name="spread",
         grid=(experts - TAIL,),
-        out_shape=finals,
+        out_shape=finals + (f32((8, LANES)),),
         in_specs=[pl.BlockSpec((2, 1, n * rows, width), lambda e: (0, e, 0, 0))],
-        out_specs=(pl.BlockSpec((1, n * rows, width), lambda e: (e, 0, 0)),) * 2,
+        out_specs=(pl.BlockSpec((1, n * rows, width), lambda e: (e, 0, 0)),) * 2
+        + (pl.BlockSpec((8, LANES), lambda e: (0, 0)),),
         cost_estimate=pl.CostEstimate(flops=0, bytes_accessed=4 * narrow.size, transcendentals=0),
     )(narrow)
+
+    routers = pl.pallas_call(
+        functools.partial(gather, n, groups),
+        name="gather",
+        out_shape=bf16((groups * share, n * tokens)),
+        in_specs=[anywhere, inside],
+        out_specs=anywhere,
+        scratch_shapes=[dma((column,)), dma((column,)), dma],
+        compiler_params=pltpu.CompilerParams(
+            collective_id=1, has_side_effects=True, vmem_limit_bytes=16 * 2**20
+        ),
+    )(token, pair)
 
     def put(name, pieces, blocks, final, small=()):
         count = len(blocks) + len(small)
@@ -421,7 +488,7 @@
     n, groups = mesh.shape["shard"], mesh.shape["expert"]
 
     def shards(gate, up, router, gain):
-        aligned = gate.shape[2] % (n * LANES) == 0 and gate.shape[1] % 16 == 0
+        aligned = gate.shape[2] % (n * LANES) == 0 and gate.shape[1] % (16 * CHUNKS) == 0
         aligned = aligned and gate.shape[0] > TAIL + SLOTS + RAMP and 2 * TAIL <= SLOTS
         aligned = aligned and router.shape[0] % LANES == 0 and router.shape[1] % 16 == 0
         if n >= 4 and n % 2 == 0 and aligned:

time: 374 us -> 371 us (level)
  waiting for transfers between devices: 13.8 us -> 2.49 us
  Pallas kernels: 357 us -> 365 us
    ppermute x2, waiting for transfers between devices: 13.8 us -> 2.49 us  [by_kernel(): lax.ppermute(ref, 'shard', [(s, shift(s, d, f, chips)) for s in range(n)])]
    pallas_call x1 -> x2, Pallas kernels: 328 us -> 336 us  [the longest x1 326 us: by_kernel(): pl.pallas_call(functools.partial(exchange, n), name='exchange', out_shape...]
  transfers between devices with their start and end apart: 2 -> 2, of which waited for: 2 -> 1; matrix products, arithmetic and copies ran while one was open for 0% -> 0% of each run, Pallas kernels for 7% -> 10%
where the time goes in v3:
time: 371 us; the launch traced here: 370 us
  Pallas kernels  365 us (98%)
    pallas_call x1, Pallas kernels, by_kernel(): pl.pallas_call(functools.partial(exchange, n), name='exchange', out_shape...  326 us
    pallas_call x1, Pallas kernels, by_kernel(): pl.pallas_call(spread, name='spread', grid=(experts - TAIL,), out_shape=f...  23.9 us
    pallas_call x1, Pallas kernels, by_kernel(): pl.pallas_call(functools.partial(gather, n, groups), name='gather', out_s...  10.3 us
  transfers between devices with their start and end apart: 2, of which 1 were waited for; matrix products, arithmetic and copies ran while one was open for 0% of the time, Pallas kernels for 10%

profile of v3, /device:TPU:1, one launch (start us, length us, event | category | flops | bytes accessed | tf_op | source)
XLA Modules:
  0.0 369.9 jit_solution(11214335990638939418)
XLA Ops:
  0.6 325.9 %exchange.1 = (bf16[2,14,2048,256]{3,2,1,0:T(8,128)(2,1)}, bf16[4,2,512,256]{3,2,1,0:T(8,128)(2,1)}, bf16[4,512,256]{2,1,0:T(8,128)(2,1)}, bf16[4,512,256]{2,1,0...) custom-call(f32[16,512,1024]{2,1,0:T(8,128)} %gate.1, f32[16,512,1024]{2,1,0:T(8,128)} %up.1, ...), custom_call_target="tpu_custom_call" | custom-call | tf_op jit(solution)/shard_map/exchange/pallas_call | solution.py:369
  326.6 0.0 copy-start.1
  326.6 0.0 copy-start
  326.6 0.0 copy-start.2
  326.6 0.0 copy-start.3
  326.6 1.3 collective-permute-start.1
  327.9 0.0 collective-permute-start
  327.9 23.9 %spread.1 = (bf16[16,2048,256]{2,1,0:T(8,128)(2,1)}, bf16[16,2048,256]{2,1,0:T(8,128)(2,1)}, f32[8,128]{1,0:T(8,128)}) custom-call(bf16[2,14,2048,256]{3,2,1,0:T(8,128)(2,1)} %get-tuple-element.27.narrow), custom_call_target="tpu_custom_call" | custom-call | bytes 58720256 | tf_op jit(solution)/shard_map/spread/pallas_call | solution.py:422
  351.8 0.0 copy-done.1
  351.8 0.0 copy-start.4
  351.8 0.7 copy-done.4
  352.5 10.3 %gather.1.refs_4_ = bf16[64,2048]{1,0:T(8,128)(2,1)S(1)} custom-call(f32[8,128]{1,0:T(8,128)S(1)} %copy-done.4, bf16[2,16,512]{2,1,0:T(8,128)(2,1)S(1)} %copy-done.1), custom_call_target="tpu_custom_call" | custom-call | tf_op jit(solution)/shard_map/gather/pallas_call | solution.py:433
  362.8 0.0 collective-permute-done.1
  362.8 0.0 copy-done
  362.8 0.0 copy-done.2
  362.8 0.0 copy-done.3
  362.8 3.6 finish_near.1
  366.4 2.5 collective-permute-done
  368.9 1.0 finish_far.1
Async XLA Ops:
  326.6 25.2 %copy-start.1 = (bf16[2,16,512]{2,1,0:T(8,128)(2,1)S(1)}, bf16[2,16,512]{2,1,0:T(8,128)(2,1)}, u32[]{:S(2)}) copy-start(bf16[2,16,512]{2,1,0:T(8,128)(2,1)} %get-tuple-element.29.pair) | copy-start | bytes 98308
  326.6 36.2 %copy-start = (bf16[4,2,512,256]{3,2,1,0:T(8,128)(2,1)S(1)}, bf16[4,2,512,256]{3,2,1,0:T(8,128)(2,1)}, u32[]{:S(2)}) copy-start(bf16[4,2,512,256]{3,2,1,0:T(8,128)(2,1)} %get-tuple-element.23.refs_0_) | copy-start | bytes 6291460
  326.6 36.2 %copy-start.2 = (f32[16,256]{1,0:T(8,128)S(1)}, f32[16,256]{1,0:T(8,128)}, u32[]{:S(2)}) copy-start(f32[16,256]{1,0:T(8,128)} %get-tuple-element.25.refs_2_) | copy-start | bytes 49156
  326.6 36.2 %copy-start.3 = (f32[16,256]{1,0:T(8,128)S(1)}, f32[16,256]{1,0:T(8,128)}, u32[]{:S(2)}) copy-start(f32[16,256]{1,0:T(8,128)} %get-tuple-element.26.refs_3_) | copy-start | bytes 49156
  326.6 36.2 %collective-permute-start.1 = (bf16[4,512,256]{2,1,0:T(8,128)(2,1)}, bf16[4,512,256]{2,1,0:T(8,128)(2,1)}, u32[]{:S(2)}, u32[]{:S(2)}) collective-permute-start(bf16[4,512,256]{2,1,0:T(8,128)(2,1)} %get-tuple-element.24), channel_id=1, source_target_pairs={{0,2},{1,3},{2,0},{3,1},{4,6},{5,7},{6,4},{7,5},{8,10},{9,11},{10,... | collective-permute-start | bytes 3145736 | tf_op jit(solution)/shard_map/ppermute | solution.py:418
  327.9 41.0 %collective-permute-start = (bf16[4,512,256]{2,1,0:T(8,128)(2,1)}, bf16[4,512,256]{2,1,0:T(8,128)(2,1)S(1)}, u32[]{:S(2)}, u32[]{:S(2)}) collective-permute-start(bf16[4,512,256]{2,1,0:T(8,128)(2,1)} %get-tuple-element.22), channel_id=1, source_target_pairs={{0,3},{1,2},{2,1},{3,0},{4,7},{5,6},{6,5},{7,4},{8,11},{9,10},{10,... | collective-permute-start | bytes 3145736 | tf_op jit(solution)/shard_map/ppermute | solution.py:418
  351.8 0.7 copy-start.4

commit v4 on v3

--- a/solution.py
+++ b/solution.py
@@ -7,35 +7,48 @@
 from jax.experimental.pallas import tpu as pltpu
 from jax.sharding import PartitionSpec as P
 
+
 MESH = pl.DeviceIdType.MESH
 LANES = 128
 TAIL = 2
+EARLY = 3
 RAMP = 3
 AHEAD = 3
 SLOTS = 6
 CHUNKS = 4
+EIGHTH = 8
 
 
 def shift(shard, d, f, chips):
     return 2 * ((shard // 2 + d) % chips) + (shard % 2 + f) % 2
+
+
+def tail_pieces(n):
+    ahead = range(1, n // 2)
+    return (
+        [(d, 0, 0, EARLY) for d in ahead]
+        + [(d, 1, 0, 2 * TAIL) for d in ahead]
+        + [(d, 0, EARLY, 2 * TAIL - EARLY) for d in ahead]
+    )
 
 
 def exchange(n, gate, up, router, gain, *refs):
     chips = n // 2
     away = [(d, f) for d in range(1, chips) for f in (0, 1)]
     same, other = [p for p in away if p[1] == 0], [p for p in away if p[1] == 1]
-    narrow, near, *far = refs[: 2 + len(away)]
+    pieces = tail_pieces(n)
+    narrow, near, *far = refs[: 2 + len(pieces)]
     (
         scale_gate, scale_up, pair, held, out, weight, by, part, scales, mine, beside, whole, cross,
-        full, direct, first_sem, load_sem, near_send, near_recv, cross_send, cross_recv, full_send,
+        full, direct, raw, late, first_sem, load_sem, near_send, near_recv, cross_send, cross_recv, full_send,
         full_recv, direct_send, direct_recv, send_sem, recv_sem, keep_sem, tail_recv, small_sem,
-        pass_send, pass_recv, scale_sem, go,
-    ) = refs[2 + len(away) :]
+        pass_send, pass_recv, scale_sem, raw_send, raw_recv, late_sem, go,
+    ) = refs[2 + len(pieces) :]
     me = lax.axis_index("shard")
     core = lax.rem(me, 2)
     items, rows, width, depth = 2 * gate.shape[0], gate.shape[1], out.shape[3], held.shape[0]
     blocks, per, half = gate.shape[2] // LANES, width // LANES, gate.shape[2] // LANES // 2
-    last, chunk = items - near.shape[0], rows // CHUNKS
+    last, chunk, wide = items - near.shape[0], rows // CHUNKS, raw.shape[1]
 
     def peer(d, f):
         return 2 * lax.rem(me // 2 + d, chips) + lax.rem(core + f, 2)
@@ -104,26 +117,47 @@
         full[k, core] = most
         remote(full.at[k, core], full.at[k, core], full_send, full_recv.at[k], device(0, 1)).start()
 
-    def place(k):
-        return narrow.at[lax.rem(k, 2), k // 2, pl.ds(pl.multiple_of(me * rows, rows), rows)]
-
-    def send(k, pieces):
+    def place(k, top=0):
+        at = pl.ds(pl.multiple_of(me * rows + top, 16), rows - top)
+        return narrow.at[lax.rem(k, 2), k // 2, at]
+
+    def send_from(k, pieces, top):
         slot = lax.rem(k, SLOTS)
         for d, f in pieces:
             remote(
-                out.at[slot, peer(d, f)], place(k), send_sem.at[slot],
-                recv_sem.at[2 * d + f - 1], device(d, f),
+                out.at[slot, peer(d, f), pl.ds(top, rows - top)], place(k, top),
+                send_sem.at[slot], recv_sem.at[jnp.minimum(k // 2, 1), 2 * d + f - 1],
+                device(d, f),
             ).start()
+
+    def send(k, pieces):
+        @pl.when(k == 0)
+        def _():
+            send_from(0, pieces, wide)
+
+        @pl.when(k > 0)
+        def _():
+            send_from(k, pieces, 0)
 
     def keep(k):
         slot = lax.rem(k, SLOTS)
-        send(k, [(0, 1)])
+        send_from(k, [(0, 1)], 0)
         pltpu.make_async_copy(out.at[slot, me], place(k), keep_sem.at[slot]).start()
+
+    def first_sent():
+        await_bytes(narrow.at[0, 0, pl.ds(0, (n - 1) * rows - len(away) * wide)], send_sem.at[0])
+        await_bytes(out.at[0, 0], keep_sem.at[0])
 
     def sent(k):
         slot = lax.rem(k, SLOTS)
         await_bytes(out.at[slot, pl.ds(0, n - 1)], send_sem.at[slot])
         await_bytes(out.at[slot, 0], keep_sem.at[slot])
+
+    def lately(j):
+        d, f = away[j]
+        source = peer(chips - d, f)
+        to = narrow.at[0, 0, pl.ds(pl.multiple_of(source * rows, rows), wide)]
+        return pltpu.make_async_copy(late.at[j], to, late_sem.at[j])
 
     def leave(k):
         slot, i = lax.rem(k, SLOTS), k - last
@@ -131,8 +165,12 @@
             out.at[slot, peer(0, 1)], near.at[i, core], send_sem.at[slot], tail_recv, device(0, 1)
         ).start()
         pltpu.make_async_copy(out.at[slot, me], near.at[i, core], keep_sem.at[slot]).start()
-        for (d, f), ref in zip(away, far):
-            pltpu.make_async_copy(out.at[slot, peer(d, f)], ref.at[i], keep_sem.at[slot]).start()
+        for (d, f, first_item, count), ref in zip(pieces, far):
+            @pl.when((i >= first_item) & (i < first_item + count))
+            def _():
+                pltpu.make_async_copy(
+                    out.at[slot, peer(d, f)], ref.at[i - first_item], keep_sem.at[slot]
+                ).start()
 
     def left(k):
         slot = lax.rem(k, SLOTS)
@@ -164,6 +202,11 @@
     pl.semaphore_wait(barrier, n - 1)
     for j, (d, f) in enumerate(away + [(0, 1)]):
         remote(mine.at[0], direct.at[j], direct_send, direct_recv, device(d, f)).start()
+    for j, (d, f) in enumerate(away):
+        columns = pl.ds(pl.multiple_of(peer(d, f) * width, width), width)
+        remote(
+            held.at[0, pl.ds(0, wide), columns], raw.at[j], raw_send, raw_recv, device(d, f)
+        ).start()
     local(1)
     load(jnp.int32(AHEAD + 1))
     tell(1)
@@ -182,7 +225,11 @@
         def _():
             await_bytes(full.at[q, 0], full_recv.at[q])
 
-        @pl.when((q > SLOTS) | ((q == SLOTS) & (core == 1)))
+        @pl.when((q == SLOTS) & (core == 1))
+        def _():
+            first_sent()
+
+        @pl.when(q > SLOTS)
         def _():
             sent(q - SLOTS)
 
@@ -225,9 +272,13 @@
         def _():
             relay(q + 1)
 
+        @pl.when(q == 0)
+        def _():
+            await_bytes(raw, raw_send)
+
         @pl.when((q == 1) & (core == 0))
         def _():
-            sent(0)
+            first_sent()
             pl.semaphore_signal(go, inc=1, device_id=device(0, 1), device_id_type=MESH)
 
         @pl.when((q == 1) & (core == 1))
@@ -245,6 +296,15 @@
 
         @pl.when(q == RAMP)
         def _():
+            await_bytes(raw, raw_recv)
+            for i in range(per):
+                b = me * per + i
+                scale = full[0, b // half, pl.ds(lax.rem(b, half), 1), :]
+                at = slice(i * LANES, (i + 1) * LANES)
+                for j in range(len(away)):
+                    late[j, :, at] = (raw[j, :, at] / scale).astype(jnp.bfloat16)
+            for j in range(len(away)):
+                lately(j).start()
             pltpu.make_async_copy(part, pair.at[0], small_sem.at[0]).start()
             for d in range(1, chips):
                 remote(part, pair.at[d], pass_send, pass_recv, device(d, 0)).start()
@@ -286,8 +346,12 @@
     for which in (0, 1):
         await_bytes(scales.at[which], scale_sem.at[which])
     await_bytes(near.at[:, 0], tail_recv)
-    for j in range(n - 1):
-        await_bytes(narrow.at[:, :, pl.ds(0, rows)], recv_sem.at[j])
+    for j in range(len(away)):
+        lately(j).wait()
+    for d, f in away + [(0, 1)]:
+        j, less = 2 * d + f - 1, wide if d > 0 else 0
+        await_bytes(narrow.at[0, 0, pl.ds(0, 2 * rows - less)], recv_sem.at[0, j])
+        await_bytes(narrow.at[:, pl.ds(1, last // 2 - 1), pl.ds(0, rows)], recv_sem.at[1, j])
 
 
 def gather(n, groups, token, pair, routers, send_sem, recv_sem, keep_sem):
@@ -335,15 +399,16 @@
     )
     gate, up, *copies = results
     me, chips = lax.axis_index("shard"), n // 2
-    experts, tail, rows = gate.shape[0], arrived[0].shape[0], gate.shape[1] // n
+    experts, rows = gate.shape[0], gate.shape[1] // n
     for at, (piece, ref) in enumerate(zip(pieces, arrived)):
-        for i in range(tail):
-            final = (gate, up)[i % 2].at[experts - tail // 2 + i // 2]
+        d, f, first_item, count = piece
+        for i in range(count):
+            item = first_item + i
+            final = (gate, up)[item % 2].at[experts - TAIL + item // 2]
             for c in range(ref.shape[1]):
-                if piece is None:
+                if d == 0:
                     source = 2 * (me // 2) + c
                 else:
-                    d, f = piece
                     source = 2 * lax.rem(me // 2 + chips - d, chips) + lax.rem(me % 2 + f, 2)
                 to = final.at[pl.ds(pl.multiple_of(source * rows, rows), rows)]
                 pltpu.make_async_copy(ref.at[i, c], to, sems.at[at]).start()
@@ -358,8 +423,7 @@
     width, items, depth, chips = columns // n, 2 * experts, RAMP + AHEAD + 2, n // 2
     tokens, share = router.shape
     half = columns // LANES // 2
-    away = [(d, f) for d in range(1, chips) for f in (0, 1)]
-    column = 2 * groups - 1
+    pieces, column = tail_pieces(n), 2 * groups - 1
     f32 = functools.partial(jax.ShapeDtypeStruct, dtype=jnp.float32)
     anywhere = pl.BlockSpec(memory_space=pl.ANY)
     inside = pl.BlockSpec(memory_space=pltpu.VMEM)
@@ -372,13 +436,13 @@
         out_shape=(
             bf16((2, experts - TAIL, n * rows, width)),
             bf16((2 * TAIL, 2, rows, width)),
-            *[bf16((2 * TAIL, rows, width)) for _ in away],
+            *[bf16((count, rows, width)) for *_, count in pieces],
             f32((experts, width)),
             f32((experts, width)),
             bf16((chips, share, tokens)),
         ),
         in_specs=[anywhere] * 4,
-        out_specs=(anywhere,) * (5 + len(away)),
+        out_specs=(anywhere,) * (5 + len(pieces)),
         scratch_shapes=[
             pltpu.VMEM((depth, rows, columns), jnp.float32),
             pltpu.VMEM((SLOTS, n, rows, width), jnp.bfloat16),
@@ -392,6 +456,8 @@
             pltpu.VMEM((items, chips - 1, half, LANES), jnp.float32),
             maxima,
             pltpu.VMEM((n - 1, 2, half, LANES), jnp.float32),
+            pltpu.VMEM((n - 2, rows // EIGHTH, width), jnp.float32),
+            pltpu.VMEM((n - 2, rows // EIGHTH, width), jnp.bfloat16),
             dma((CHUNKS,)),
             dma((depth,)),
             dma,
@@ -403,21 +469,23 @@
             dma,
             dma,
             dma((SLOTS,)),
-            dma((n - 1,)),
+            dma((2, n - 1)),
             dma((SLOTS,)),
             dma,
             dma((2,)),
             dma,
             dma,
             dma((2,)),
+            dma,
+            dma,
+            dma((n - 2,)),
             pltpu.SemaphoreType.REGULAR,
         ],
         compiler_params=pltpu.CompilerParams(collective_id=0, has_side_effects=True),
     )(gate, up, router.T, gain.reshape(1, tokens))
-    arrived = [
-        lax.ppermute(ref, "shard", [(s, shift(s, d, f, chips)) for s in range(n)])
-        for (d, f), ref in zip(away, far)
-    ]
+    arrived = []
+    for (d, f, *_), ref in zip(pieces, far):
+        arrived.append(lax.ppermute(ref, "shard", [(s, shift(s, d, f, chips)) for s in range(n)]))
     finals = (bf16((experts, n * rows, width)),) * 2
     *final, token = pl.pallas_call(
         spread,
@@ -428,6 +496,7 @@
         out_specs=(pl.BlockSpec((1, n * rows, width), lambda e: (e, 0, 0)),) * 2
         + (pl.BlockSpec((8, LANES), lambda e: (0, 0)),),
         cost_estimate=pl.CostEstimate(flops=0, bytes_accessed=4 * narrow.size, transcendentals=0),
+        compiler_params=pltpu.CompilerParams(vmem_limit_bytes=24 * 2**20),
     )(narrow)
 
     routers = pl.pallas_call(
@@ -442,11 +511,10 @@
         ),
     )(token, pair)
 
-    def put(name, pieces, blocks, final, small=()):
+    def put(pieces, blocks, final, small=()):
         count = len(blocks) + len(small)
         return pl.pallas_call(
             functools.partial(finish, n, pieces, len(small)),
-            name=name,
             out_shape=finals + tuple(jax.ShapeDtypeStruct(s.shape, s.dtype) for s in small),
             in_specs=[inside] * count + [anywhere] * 2,
             out_specs=(anywhere,) * 2 + (inside,) * len(small),
@@ -456,11 +524,13 @@
         )(*blocks, *small, *final)
 
     blocks = [jnp.expand_dims(ref, 1) for ref in arrived]
+    third = len(pieces) // 3
     *final, scale_gate, scale_up, routers = put(
-        "finish_near", [None] + away[:-1], [near] + blocks[:-1], final,
+        [(0, 0, 0, 2 * TAIL)] + pieces[:third], [near] + blocks[:third], final,
         (scale_gate, scale_up, routers),
     )
-    final_gate, final_up = put("finish_far", away[-1:], blocks[-1:], final)
+    final = put(pieces[third:-third], blocks[third:-third], final)
+    final_gate, final_up = put(pieces[-third:], blocks[-third:], final)
     return final_gate, final_up, scale_gate, scale_up, routers.T
 
 
@@ -488,7 +558,7 @@
     n, groups = mesh.shape["shard"], mesh.shape["expert"]
 
     def shards(gate, up, router, gain):
-        aligned = gate.shape[2] % (n * LANES) == 0 and gate.shape[1] % (16 * CHUNKS) == 0
+        aligned = gate.shape[2] % (n * LANES) == 0 and gate.shape[1] % (16 * CHUNKS * EIGHTH) == 0
         aligned = aligned and gate.shape[0] > TAIL + SLOTS + RAMP and 2 * TAIL <= SLOTS
         aligned = aligned and router.shape[0] % LANES == 0 and router.shape[1] % 16 == 0
         if n >= 4 and n % 2 == 0 and aligned:

time: 371 us -> 374 us (level)
  Pallas kernels: 365 us -> 351 us
  local copies, waits for them, and re-layouts: 0.7 us -> 9.37 us
  waiting for transfers between devices: 2.49 us -> 9.13 us
    pallas_call x1, Pallas kernels: 23.9 us -> 11.7 us  [by_kernel(): pl.pallas_call(spread, name='spread', grid=(experts - TAIL,), out_shape=f...]
    unnamed x10, local copies, waits for them, and re-layouts: 0.7 us -> 9.37 us
    ppermute x2 -> x3, waiting for transfers between devices: 2.49 us -> 9.13 us  [by_kernel(): lax.ppermute(ref, 'shard', [(s, shift(s, d, f, chips)) for s in range(n)])]
  transfers between devices with their start and end apart: 2 -> 3, of which waited for: 1 -> 2; matrix products, arithmetic and copies ran while one was open for 0% -> 0% of each run, Pallas kernels for 10% -> 7%
where the time goes in v4:
time: 374 us; the launch traced here: 372 us
  Pallas kernels  351 us (94%)
  local copies, waits for them, and re-layouts  9.37 us (3%)
  waiting for transfers between devices  9.13 us (2%)
    pallas_call x1, Pallas kernels, by_kernel(): pl.pallas_call(functools.partial(exchange, n), name='exchange', out_shape...  324 us
    pallas_call x1, Pallas kernels, by_kernel(): pl.pallas_call(functools.partial(gather, n, groups), name='gather', out_s...  11.7 us
    pallas_call x1, Pallas kernels, by_kernel(): pl.pallas_call(spread, name='spread', grid=(experts - TAIL,), out_shape=f...  11.7 us
    unnamed x10, local copies, waits for them, and re-layouts  9.37 us
    ppermute x3, waiting for transfers between devices, by_kernel(): lax.ppermute(ref, 'shard', [(s, shift(s, d, f, chips)) for s in range(n)])  9.13 us
  transfers between devices with their start and end apart: 3, of which 2 were waited for; matrix products, arithmetic and copies ran while one was open for 0% of the time, Pallas kernels for 7%

profile of v4, /device:TPU:1, one launch (start us, length us, event | category | flops | bytes accessed | tf_op | source)
XLA Modules:
  0.0 372.2 jit_solution(2432619393920794800)
XLA Ops:
  0.6 323.9 %exchange.1 = (bf16[2,14,2048,256]{3,2,1,0:T(8,128)(2,1)}, bf16[4,2,512,256]{3,2,1,0:T(8,128)(2,1)}, bf16[3,512,256]{2,1,0:T(8,128)(2,1)}, bf16[4,512,256]{2,1,0...) custom-call(f32[16,512,1024]{2,1,0:T(8,128)} %gate.1, ...), custom_call_target="tpu_custom_call" | custom-call | tf_op jit(solution)/shard_map/exchange/pallas_call | solution.py:433
  324.6 0.1 collective-permute-start.1
  324.6 1.3 collective-permute-start.2
  326.0 0.2 collective-permute-start
  326.2 0.0 copy-start
  326.2 9.3 %copy-done = bf16[2,14,2048,256]{3,2,1,0:T(8,128)(2,1)S(1)} copy-done((bf16[2,14,2048,256]{3,2,1,0:T(8,128)(2,1)S(1)}, bf16[2,14,2048,256]{3,2,1,0:T(8,128)(2,1)}, u32[]{:S(2)}) %copy-start) | copy-done | bytes 29360152
  335.5 0.0 copy-start.2
  335.5 0.0 copy-start.1
  335.5 0.0 copy-start.3
  335.5 0.0 copy-start.4
  335.5 11.7 %spread.1 = (bf16[16,2048,256]{2,1,0:T(8,128)(2,1)}, bf16[16,2048,256]{2,1,0:T(8,128)(2,1)}, f32[8,128]{1,0:T(8,128)S(1)}) custom-call(bf16[2,14,2048,256]{3,2,1,0:T(8,128)(2,1)S(1)} %copy-done), custom_call_target="tpu_custom_call" | custom-call | bytes 58720256 | tf_op jit(solution)/shard_map/spread/pallas_call | solution.py:490
  347.3 0.0 copy-done.2
  347.3 11.7 %gather.1.refs_4_ = bf16[64,2048]{1,0:T(8,128)(2,1)S(1)} custom-call(f32[8,128]{1,0:T(8,128)S(1)} %get-tuple-element.32.token, bf16[2,16,512]{2,1,0:T(8,128)(2,1)S(1)} %copy-done.2), custom_call_target="tpu_custom_call" | custom-call | tf_op jit(solution)/shard_map/gather/pallas_call | solution.py:502
  359.0 6.9 %collective-permute-done.2 = bf16[3,512,256]{2,1,0:T(8,128)(2,1)S(1)} collective-permute-done((bf16[3,512,256]{2,1,0:T(8,128)(2,1)}, bf16[3,512,256]{2,1,0:T(8,128)(2,1)S(1)}, u32[]{:S(2)}, u32[]{:S(2)}) %collective-permute-start.2) | collective-permute-done | bytes 786464 | tf_op jit(solution)/shard_map/ppermute | solution.py:488
  365.9 0.0 copy-done.1
  365.9 0.0 copy-done.3
  365.9 0.0 copy-done.4
  365.9 2.3 shard_map.83
  368.2 0.0 collective-permute-done.1
  368.2 1.0 shard_map.84
  369.2 2.3 collective-permute-done
  371.5 0.7 shard_map.85
Async XLA Ops:
  324.6 43.6 %collective-permute-start.1 = (bf16[4,512,256]{2,1,0:T(8,128)(2,1)}, bf16[4,512,256]{2,1,0:T(8,128)(2,1)S(1)}, u32[]{:S(2)}, u32[]{:S(2)}) collective-permute-start(bf16[4,512,256]{2,1,0:T(8,128)(2,1)} %get-tuple-element.26), channel_id=1, source_target_pairs={{0,3},{1,2},{2,1},{3,0},{4,7},{5,6},{6,5},{7,4},{8,11},{9,10},{10,... | collective-permute-start | bytes 3145736 | tf_op jit(solution)/shard_map/ppermute | solution.py:488
  324.6 41.2 %collective-permute-start.2 = (bf16[3,512,256]{2,1,0:T(8,128)(2,1)}, bf16[3,512,256]{2,1,0:T(8,128)(2,1)S(1)}, u32[]{:S(2)}, u32[]{:S(2)}) collective-permute-start(bf16[3,512,256]{2,1,0:T(8,128)(2,1)} %get-tuple-element.28), channel_id=1, source_target_pairs={{0,2},{1,3},{2,0},{3,1},{4,6},{5,7},{6,4},{7,5},{8,10},{9,11},{10,... | collective-permute-start | bytes 2359304 | tf_op jit(solution)/shard_map/ppermute | solution.py:488
  326.0 45.5 %collective-permute-start = (bf16[1,512,256]{2,1,0:T(8,128)(2,1)}, bf16[1,512,256]{2,1,0:T(8,128)(2,1)S(1)}, u32[]{:S(2)}, u32[]{:S(2)}) collective-permute-start(bf16[1,512,256]{2,1,0:T(8,128)(2,1)} %get-tuple-element.25), channel_id=1, source_target_pairs={{0,2},{1,3},{2,0},{3,1},{4,6},{5,7},{6,4},{7,5},{8,10},{9,11},{10,... | collective-permute-start | bytes 786440 | tf_op jit(solution)/shard_map/ppermute | solution.py:488
  326.2 9.4 %copy-start = (bf16[2,14,2048,256]{3,2,1,0:T(8,128)(2,1)S(1)}, bf16[2,14,2048,256]{3,2,1,0:T(8,128)(2,1)}, u32[]{:S(2)}) copy-start(bf16[2,14,2048,256]{3,2,1,0:T(8,128)(2,1)} %get-tuple-element.31.narrow) | copy-start | bytes 88080384
  335.5 11.7 %copy-start.2 = (bf16[2,16,512]{2,1,0:T(8,128)(2,1)S(1)}, bf16[2,16,512]{2,1,0:T(8,128)(2,1)}, u32[]{:S(2)}) copy-start(bf16[2,16,512]{2,1,0:T(8,128)(2,1)} %get-tuple-element.33.pair) | copy-start | bytes 98308
  335.5 30.3 %copy-start.1 = (bf16[4,2,512,256]{3,2,1,0:T(8,128)(2,1)S(1)}, bf16[4,2,512,256]{3,2,1,0:T(8,128)(2,1)}, u32[]{:S(2)}) copy-start(bf16[4,2,512,256]{3,2,1,0:T(8,128)(2,1)} %get-tuple-element.27.refs_0_) | copy-start | bytes 6291460
  335.5 30.3 %copy-start.3 = (f32[16,256]{1,0:T(8,128)S(1)}, f32[16,256]{1,0:T(8,128)}, u32[]{:S(2)}) copy-start(f32[16,256]{1,0:T(8,128)} %get-tuple-element.29.refs_2_) | copy-start | bytes 49156
  335.5 30.3 %copy-start.4 = (f32[16,256]{1,0:T(8,128)S(1)}, f32[16,256]{1,0:T(8,128)}, u32[]{:S(2)}) copy-start(f32[16,256]{1,0:T(8,128)} %get-tuple-element.30.refs_3_) | copy-start | bytes 49156

commit v5 on v4

--- a/solution.py
+++ b/solution.py
@@ -14,7 +14,7 @@
 EARLY = 3
 RAMP = 3
 AHEAD = 3
-SLOTS = 6
+SLOTS = 8
 CHUNKS = 4
 EIGHTH = 8
 
@@ -303,11 +303,14 @@
                 at = slice(i * LANES, (i + 1) * LANES)
                 for j in range(len(away)):
                     late[j, :, at] = (raw[j, :, at] / scale).astype(jnp.bfloat16)
-            for j in range(len(away)):
-                lately(j).start()
             pltpu.make_async_copy(part, pair.at[0], small_sem.at[0]).start()
             for d in range(1, chips):
                 remote(part, pair.at[d], pass_send, pass_recv, device(d, 0)).start()
+
+        @pl.when(q == RAMP + 1)
+        def _():
+            for j in range(len(away)):
+                lately(j).start()
 
         return 0
 
@@ -558,7 +561,8 @@
     n, groups = mesh.shape["shard"], mesh.shape["expert"]
 
     def shards(gate, up, router, gain):
-        aligned = gate.shape[2] % (n * LANES) == 0 and gate.shape[1] % (16 * CHUNKS * EIGHTH) == 0
+        aligned = gate.shape[2] % (n * LANES) == 0 and gate.shape[1] % (16 * CHUNKS) == 0
+        aligned = aligned and gate.shape[1] % (16 * EIGHTH) == 0
         aligned = aligned and gate.shape[0] > TAIL + SLOTS + RAMP and 2 * TAIL <= SLOTS
         aligned = aligned and router.shape[0] % LANES == 0 and router.shape[1] % 16 == 0
         if n >= 4 and n % 2 == 0 and aligned:

time: 374 us -> 374 us (level)
  no operation moved by 1% of the time
where the time goes in v5:
time: 374 us; the launch traced here: 372 us
  Pallas kernels  351 us (94%)
  local copies, waits for them, and re-layouts  9.37 us (3%)
  waiting for transfers between devices  9.13 us (2%)
    pallas_call x1, Pallas kernels, by_kernel(): pl.pallas_call(functools.partial(exchange, n), name='exchange', out_shape...  324 us
    pallas_call x1, Pallas kernels, by_kernel(): pl.pallas_call(functools.partial(gather, n, groups), name='gather', out_s...  11.7 us
    pallas_call x1, Pallas kernels, by_kernel(): pl.pallas_call(spread, name='spread', grid=(experts - TAIL,), out_shape=f...  11.7 us
    unnamed x10, local copies, waits for them, and re-layouts  9.37 us
    ppermute x3, waiting for transfers between devices, by_kernel(): lax.ppermute(ref, 'shard', [(s, shift(s, d, f, chips)) for s in range(n)])  9.13 us
  transfers between devices with their start and end apart: 3, of which 2 were waited for; matrix products, arithmetic and copies ran while one was open for 0% of the time, Pallas kernels for 7%

profile of v5, /device:TPU:1, one launch (start us, length us, event | category | flops | bytes accessed | tf_op | source)
XLA Modules:
  0.0 372.2 jit_solution(1450515629629459273)
XLA Ops:
  0.6 324.0 %exchange.1 = (bf16[2,14,2048,256]{3,2,1,0:T(8,128)(2,1)}, bf16[4,2,512,256]{3,2,1,0:T(8,128)(2,1)}, bf16[3,512,256]{2,1,0:T(8,128)(2,1)}, bf16[4,512,256]{2,1,0...) custom-call(f32[16,512,1024]{2,1,0:T(8,128)} %gate.1, ...), custom_call_target="tpu_custom_call" | custom-call | tf_op jit(solution)/shard_map/exchange/pallas_call | solution.py:436
  324.6 0.1 collective-permute-start.1
  324.7 1.3 collective-permute-start.2
  326.0 0.2 collective-permute-start
  326.2 0.0 copy-start
  326.2 9.3 %copy-done = bf16[2,14,2048,256]{3,2,1,0:T(8,128)(2,1)S(1)} copy-done((bf16[2,14,2048,256]{3,2,1,0:T(8,128)(2,1)S(1)}, bf16[2,14,2048,256]{3,2,1,0:T(8,128)(2,1)}, u32[]{:S(2)}) %copy-start) | copy-done | bytes 29360152
  335.6 0.0 copy-start.2
  335.6 0.0 copy-start.1
  335.6 0.0 copy-start.3
  335.6 0.0 copy-start.4
  335.6 11.7 %spread.1 = (bf16[16,2048,256]{2,1,0:T(8,128)(2,1)}, bf16[16,2048,256]{2,1,0:T(8,128)(2,1)}, f32[8,128]{1,0:T(8,128)S(1)}) custom-call(bf16[2,14,2048,256]{3,2,1,0:T(8,128)(2,1)S(1)} %copy-done), custom_call_target="tpu_custom_call" | custom-call | bytes 58720256 | tf_op jit(solution)/shard_map/spread/pallas_call | solution.py:493
  347.3 0.0 copy-done.2
  347.3 11.7 %gather.1.refs_4_ = bf16[64,2048]{1,0:T(8,128)(2,1)S(1)} custom-call(f32[8,128]{1,0:T(8,128)S(1)} %get-tuple-element.32.token, bf16[2,16,512]{2,1,0:T(8,128)(2,1)S(1)} %copy-done.2), custom_call_target="tpu_custom_call" | custom-call | tf_op jit(solution)/shard_map/gather/pallas_call | solution.py:505
  359.0 6.9 %collective-permute-done.2 = bf16[3,512,256]{2,1,0:T(8,128)(2,1)S(1)} collective-permute-done((bf16[3,512,256]{2,1,0:T(8,128)(2,1)}, bf16[3,512,256]{2,1,0:T(8,128)(2,1)S(1)}, u32[]{:S(2)}, u32[]{:S(2)}) %collective-permute-start.2) | collective-permute-done | bytes 786464 | tf_op jit(solution)/shard_map/ppermute | solution.py:491
  365.9 0.0 copy-done.1
  365.9 0.0 copy-done.3
  365.9 0.0 copy-done.4
  365.9 2.3 shard_map.83
  368.2 0.0 collective-permute-done.1
  368.2 1.0 shard_map.84
  369.2 2.3 collective-permute-done
  371.5 0.7 shard_map.85
Async XLA Ops:
  324.6 43.6 %collective-permute-start.1 = (bf16[4,512,256]{2,1,0:T(8,128)(2,1)}, bf16[4,512,256]{2,1,0:T(8,128)(2,1)S(1)}, u32[]{:S(2)}, u32[]{:S(2)}) collective-permute-start(bf16[4,512,256]{2,1,0:T(8,128)(2,1)} %get-tuple-element.26), channel_id=1, source_target_pairs={{0,3},{1,2},{2,1},{3,0},{4,7},{5,6},{6,5},{7,4},{8,11},{9,10},{10,... | collective-permute-start | bytes 3145736 | tf_op jit(solution)/shard_map/ppermute | solution.py:491
  324.7 41.2 %collective-permute-start.2 = (bf16[3,512,256]{2,1,0:T(8,128)(2,1)}, bf16[3,512,256]{2,1,0:T(8,128)(2,1)S(1)}, u32[]{:S(2)}, u32[]{:S(2)}) collective-permute-start(bf16[3,512,256]{2,1,0:T(8,128)(2,1)} %get-tuple-element.28), channel_id=1, source_target_pairs={{0,2},{1,3},{2,0},{3,1},{4,6},{5,7},{6,4},{7,5},{8,10},{9,11},{10,... | collective-permute-start | bytes 2359304 | tf_op jit(solution)/shard_map/ppermute | solution.py:491
  326.0 45.5 %collective-permute-start = (bf16[1,512,256]{2,1,0:T(8,128)(2,1)}, bf16[1,512,256]{2,1,0:T(8,128)(2,1)S(1)}, u32[]{:S(2)}, u32[]{:S(2)}) collective-permute-start(bf16[1,512,256]{2,1,0:T(8,128)(2,1)} %get-tuple-element.25), channel_id=1, source_target_pairs={{0,2},{1,3},{2,0},{3,1},{4,6},{5,7},{6,4},{7,5},{8,10},{9,11},{10,... | collective-permute-start | bytes 786440 | tf_op jit(solution)/shard_map/ppermute | solution.py:491
  326.2 9.4 %copy-start = (bf16[2,14,2048,256]{3,2,1,0:T(8,128)(2,1)S(1)}, bf16[2,14,2048,256]{3,2,1,0:T(8,128)(2,1)}, u32[]{:S(2)}) copy-start(bf16[2,14,2048,256]{3,2,1,0:T(8,128)(2,1)} %get-tuple-element.31.narrow) | copy-start | bytes 88080384
  335.6 11.7 %copy-start.2 = (bf16[2,16,512]{2,1,0:T(8,128)(2,1)S(1)}, bf16[2,16,512]{2,1,0:T(8,128)(2,1)}, u32[]{:S(2)}) copy-start(bf16[2,16,512]{2,1,0:T(8,128)(2,1)} %get-tuple-element.33.pair) | copy-start | bytes 98308
  335.6 30.3 %copy-start.1 = (bf16[4,2,512,256]{3,2,1,0:T(8,128)(2,1)S(1)}, bf16[4,2,512,256]{3,2,1,0:T(8,128)(2,1)}, u32[]{:S(2)}) copy-start(bf16[4,2,512,256]{3,2,1,0:T(8,128)(2,1)} %get-tuple-element.27.refs_0_) | copy-start | bytes 6291460
  335.6 30.3 %copy-start.3 = (f32[16,256]{1,0:T(8,128)S(1)}, f32[16,256]{1,0:T(8,128)}, u32[]{:S(2)}) copy-start(f32[16,256]{1,0:T(8,128)} %get-tuple-element.29.refs_2_) | copy-start | bytes 49156
  335.6 30.3 %copy-start.4 = (f32[16,256]{1,0:T(8,128)S(1)}, f32[16,256]{1,0:T(8,128)}, u32[]{:S(2)}) copy-start(f32[16,256]{1,0:T(8,128)} %get-tuple-element.30.refs_3_) | copy-start | bytes 49156
